TPU v7x, 256 devices: a whole 4x4x8 slice. The times are simulated.
256 devices in a mesh: grp: 4 (over x), gx: 16 (over y, z_lo, core), gy: 4 (over z_hi).
Axes of the slice: x: 4, y: 4, z: 8 (z_hi: 4, z_lo: 2; z = z_hi * 2 + z_lo), core: 2. Of those that a mesh axis runs over, the one named last changes fastest.
Arguments:
- pressure_start: float32 [128, 32, 512], P('gx', 'gy', 'grp'), may hold values from -6 to 6
- saturation: float32 [128, 32, 512], P('gx', 'gy', 'grp'), may hold values from 0.1 to 0.9
- permeability: float32 [128, 32, 512], P('gx', 'gy', 'grp'), may hold values from 0.1 to 10
- rock_type: int32 [128, 32, 512], P('gx', 'gy', 'grp'), may hold values from 0 to 3
- rock_table: float32 [5, 4], replicated, may hold values from 0.5 to 3
- well_cells: int32 [64], replicated, may hold values from 0 to 2097151
- well_rates: float32 [64], replicated, may hold values from -12 to 12
- owner_map: int32 [16, 4, 4, 64, 1], P('gx', 'gy', 'grp'), may hold values from 0 to 15; in each aligned block of 64 rows (0 to 63, 64 to 127, ..., all dimensions but the last counted through in order) at most 8 rows name the same one
- stiffness: bfloat16 [16, 4, 4, 16, 8, 24, 24], P('gx', 'gy', 'grp'), may hold values from -0.008 to 0.2, as said below
- anchored: int32 [128, 32, 512], P('gx', 'gy', 'grp'), may hold values 0 or 1
Outputs:
- pressure: float32 [128, 32, 512], P('gx', 'gy', 'grp')
- vol_strain: float32 [128, 32, 512], P('gx', 'gy', 'grp')
Inputs may be any that keep to these rules, and one draw needn't show every extreme that they name: `owner_map`: of the 64 bricks of one device, at most 8 have the same owner. `stiffness`: the diagonal entries of every block lie between 0.1 and 0.2.
All inputs are finite; a program needn't handle non-finite values. No bound on the sum of `anchored` on one device may be relied on, other than what follows from the above.
Results may differ from a plain program's by a relative error of at most 0.0013.
Values may be sent and summed in bfloat16 or wider, within the bound.
No kernel may reach another device: no remote copies, remote signals or barrier semaphores. Data moves between devices by JAX's collectives and lax.ppermute only.
A program may use at most 64 MiB of HBM per device.

v0:
```python
import jax
import jax.numpy as jnp
import numpy as np
from jax import lax
from jax.experimental import pallas as pl
from jax.experimental.pallas import tpu as pltpu
from jax.sharding import Mesh
from jax.sharding import PartitionSpec as P

ITERS = 2
FLOW_PASSES = 4
MECH_PASSES = 3
OMEGA = 0.6
GX = ("gx_0", "gx_1", "gx_2")
BF = jnp.bfloat16
F32 = jnp.float32
RIM = 8
ZRIM = 14
ZR1 = 7
ERIM = 3


def row_order():
    order = np.zeros((32, 24), np.float32)
    sign = np.zeros((2, 2, 8), np.float32)
    for c in range(3):
        for dx in (0, 1):
            for dy in (0, 1):
                for dz in (0, 1):
                    order[8 * (2 * dx + dy) + 4 * dz + c, 8 * c + 4 * dx + 2 * dy + dz] = 1.0
                    sign[dx, dy, 4 * dz + c] = 0.25 * (2 * (dx, dy, dz)[c] - 1)
    return order, sign


def exchange(to_low, to_high, axis, periodic):
    count = lax.axis_size(axis)
    last = count if periodic else count - 1
    up = [(i, (i + 1) % count) for i in range(last)]
    down = [((i + 1) % count, i) for i in range(last)]
    return lax.ppermute(to_high, axis, up), lax.ppermute(to_low, axis, down)


def rows_of(*parts):
    return jnp.concatenate([p.reshape(-1, 128) for p in parts], axis=0)


def cut_rows(buffer, shapes):
    out, at = [], 0
    for shape in shapes:
        rows = int(np.prod(shape)) // 128
        out.append(buffer[at : at + rows].reshape(shape))
        at += rows
    return out


def lane_pad(a):
    return jnp.pad(a, [(0, 0)] * (a.ndim - 1) + [(0, 128 - a.shape[-1])])


def cut_along(array, dim, peers):
    lengths = array.shape
    parts = array.reshape(*lengths[:dim], peers, lengths[dim] // peers, *lengths[dim + 1 :])
    return jnp.moveaxis(parts, dim, 0)


def joined_along(parts, dim):
    lengths = list(parts.shape[1:])
    lengths[dim] *= parts.shape[0]
    return jnp.moveaxis(parts, 0, dim).reshape(lengths)


def exchange_in_order(parts, axes, order):
    lengths = [lax.axis_size(a) for a in axes]
    parts = parts.reshape(*lengths, *parts.shape[1:])
    for k in order:
        parts = lax.all_to_all(parts, axes[k], split_axis=k, concat_axis=k, tiled=True)
    return parts.reshape(-1, *parts.shape[len(axes) :])


def core_and_chips(array, groups, order, split_dim, concat_dim):
    peers = lax.axis_size(groups[0]) * lax.axis_size(groups[1])
    parts = cut_along(array, split_dim, peers)
    return joined_along(exchange_in_order(parts, groups, order), concat_dim)


def pick(rock, table):
    one_hot = (rock[None] == jnp.arange(table.shape[1], dtype=jnp.int32)[:, None, None, None]).astype(F32)
    return jnp.tensordot(table, one_hot, 1, precision=lax.Precision.HIGHEST)


def transmit(a, b):
    total = a + b
    return 2.0 * a * b / jnp.where(total > 0, total, 1.0)


def roll_up(a, axis):
    return pltpu.roll(a, a.shape[axis] - 1, axis)


def roll_down(a, axis):
    return pltpu.roll(a, 1, axis)


def flow_passes(start, spare, num, tx, ty, ty_low, tz, tz_low, inv_den, biot, load, out):
    ex = start.shape[0]
    cx, cy, width = out.shape
    for k in range(1, FLOW_PASSES + 1):
        src = start if k % 2 == 1 else spare
        dst = spare if k % 2 == 1 else start
        lo, hi = 1 + k, ex - 1 - k

        def step(x, carry):
            mid = src[x]
            total = (
                (num[x] + tx[x - 1] * src[x - 1])
                + (tx[x] * src[x + 1] + ty[x] * roll_up(mid, 0))
                + (ty_low[x] * roll_down(mid, 0) + tz[x] * roll_up(mid, 1))
                + tz_low[x] * roll_down(mid, 1)
            ) * inv_den[x]
            dst[x] = total
            if k == FLOW_PASSES:
                load[x - lo] = total * biot[x]
            return carry

        lax.fori_loop(lo, hi, step, 0, unroll=2)
    out[...] = start[RIM : RIM + cx, RIM : RIM + cy, :width]


def tile_row():
    return lax.broadcasted_iota(jnp.int32, (8, 256), 0)


def fold(g):
    swapped = pltpu.roll(g, 4, 0)
    return g + jnp.where(tile_row() < 4, roll_down(swapped, 1), roll_up(swapped, 1))


def brick_product(ko, ke, u_own, u_end):
    f_own = jnp.dot(ko, u_own, preferred_element_type=F32)
    f_end = jnp.dot(ke, u_end, preferred_element_type=F32)
    lane = lax.broadcasted_iota(jnp.int32, (32, 128), 1)
    f_end = jnp.where(lane < 64, f_end[:32], f_end[32:])
    return [jnp.concatenate([f_own[8 * q : 8 * q + 8], f_end[8 * q : 8 * q + 8]], axis=1) for q in range(4)]


def spread_rows(products, n, x, low_x, high_x):
    last = None
    for y in range(n):
        now = products(y)
        if last is not None:
            low_x[x, y - 1] = now[0] + last[1]
            high_x[x, y - 1] = now[2] + last[3]
        last = now


def elastic_static(held, k_own, k_ends, free, step, low_x, high_x):
    n = k_own.shape[0]
    eye = (lax.broadcasted_iota(jnp.int32, (64, 32), 0) % 32) == lax.broadcasted_iota(jnp.int32, (64, 32), 1)
    eye = jnp.where(eye, 1.0, 0.0)
    ones = jnp.ones((32, 128), BF)

    def bricks(x, carry):
        def product(y):
            ko = (k_own[x, y].astype(F32) * eye[:32]).astype(BF)
            ke = (k_ends[x, y].astype(F32) * eye).astype(BF)
            return brick_product(ko, ke, ones, ones)

        spread_rows(product, n, x, low_x, high_x)
        return carry

    lax.fori_loop(0, n, bricks, 0)

    def nodes(i, carry):
        m = RIM - ERIM
        for j in range(n - 1):
            diag = fold(low_x[i + 1, j] + high_x[i, j])
            near = [
                jnp.broadcast_to(held[i + m + a, j + m + b : j + m + b + 1, :], (8, 256))
                for a in (0, 1)
                for b in (0, 1)
            ]
            near = (near[0] + near[1]) + (near[2] + near[3])
            near = near + jnp.where(tile_row() < 4, roll_down(near, 1), roll_up(near, 1))
            loose = jnp.where(near > 0, 0.0, 1.0)
            free[i, j] = loose
            step[i, j] = jnp.where(diag > 0, OMEGA * loose / jnp.where(diag > 0, diag, 1.0), 0.0)
        return carry

    lax.fori_loop(0, n - 1, nodes, 0)


def elastic_load(bp, signs, load):
    n = bp.shape[0]
    m = RIM - ERIM

    def nodes(i, carry):
        sign = [signs[q] for q in range(4)]
        for j in range(n - 1):
            total = None
            for dx in (0, 1):
                for dy in (0, 1):
                    y = j + m + 1 - dy
                    term = jnp.broadcast_to(bp[i + 1 - dx, y : y + 1, :], (8, 256)) * sign[2 * dx + dy]
                    total = term if total is None else total + term
            load[i, j] = fold(total)
        return carry

    lax.fori_loop(0, n - 1, nodes, 0)


def elastic_pass(rim, disp, load, free, step, k_own, k_ends, low_x, high_x, cx):
    n, m = cx + 2 * rim, ERIM - rim

    def bricks(x, carry):
        def product(y):
            u = jnp.concatenate([disp[x + m + dx, y + m + dy] for dx in (0, 1) for dy in (0, 1)], axis=0).astype(BF)
            return brick_product(k_own[x + m, y + m], k_ends[x + m, y + m], u[:, :128], u[:, 128:])

        spread_rows(product, n, x, low_x, high_x)
        return carry

    lax.fori_loop(0, n, bricks, 0)

    def nodes(i, carry):
        for j in range(n - 1):
            residual = load[i + m, j + m] - fold(low_x[i + 1, j] + high_x[i, j])
            at = (i + m + 1, j + m + 1)
            disp[at] = free[i + m, j + m] * disp[at] + step[i + m, j + m] * residual
        return carry

    lax.fori_loop(0, n - 1, nodes, 0)


def elastic_strain(disp, signs, out):
    cx, cy, width = out.shape

    def cells(x, carry):
        sign = [signs[q] for q in range(4)]
        for y in range(cy):
            total = None
            for dx in (0, 1):
                for dy in (0, 1):
                    term = disp[x + ERIM + dx, y + ERIM + dy] * sign[2 * dx + dy]
                    total = term if total is None else total + term
            out[x, y : y + 1, :] = jnp.sum(total, axis=0, keepdims=True)[:, :width]
        return carry

    lax.fori_loop(0, cx, cells, 0)


def first_flow(
    table, z_range, fp, fc, fr, fh, ends, place, p_own, c_own, source, k_own, k_ends, signs,
    out, strain, packed, base, stress, biot, tx, ty, ty_low, tz, tz_low, inv_den, free, step,
    start, spare, cond, num, held, bp, disp, load, low_x, high_x,
):
    ex, ey = start.shape[0], start.shape[1]
    cx = p_own.shape[0]
    lane = lax.broadcasted_iota(jnp.int32, (ey, 256), 1)
    z_at = jnp.where(lane < 192, lane, lane - 256) + z_range[0]
    z_in = (z_at >= 0) & (z_at < z_range[1])

    def choose(rock, row):
        value = jnp.full(rock.shape, table[row, 3], F32)
        for r in range(3):
            value = jnp.where(rock == float(r), table[row, r], value)
        return value

    def gather(x, carry):
        apart = jnp.dot(ends[x], place[...], preferred_element_type=F32)
        start[x] = jnp.concatenate([fp[x].astype(F32), apart[:, :128]], axis=1)
        cond[x] = jnp.concatenate([fc[x].astype(F32), apart[:, 128:256]], axis=1)
        rock = jnp.concatenate([fr[x].astype(F32), apart[:, 256:384]], axis=1)
        held[x] = jnp.concatenate([fh[x].astype(F32), apart[:, 384:]], axis=1)
        storage = choose(rock, 2)
        strained = choose(rock, 3)
        base[x] = storage
        stress[x] = strained
        biot[x] = jnp.where(z_in, choose(rock, 4), 0.0)
        inv_den[x] = storage + strained
        return carry

    lax.fori_loop(0, ex, gather, 0, unroll=2)
    start[RIM : RIM + cx, RIM : RIM + p_own.shape[1], 0:128] = p_own[...]
    cond[RIM : RIM + cx, RIM : RIM + p_own.shape[1], 0:128] = c_own[...]

    def static_terms(x, carry):
        c = cond[x]
        tx[x] = transmit(c, cond[jnp.minimum(x + 1, ex - 1)])
        t = transmit(c, roll_up(c, 0))
        low = roll_down(t, 0)
        ty[x] = t
        ty_low[x] = low
        den = inv_den[x] + t + low
        t = transmit(c, roll_up(c, 1))
        low = roll_down(t, 1)
        tz[x] = t
        tz_low[x] = low
        p = start[x]
        b = base[x] * p + source[x]
        base[x] = b
        num[x] = b + stress[x] * p
        inv_den[x] = 1.0 / (den + t + low + tx[x] + tx[jnp.maximum(x - 1, 0)])
        return carry

    lax.fori_loop(0, ex, static_terms, 0, unroll=2)
    flow_passes(start, spare, num, tx, ty, ty_low, tz, tz_low, inv_den, biot, bp, out)
    elastic_static(held, k_own, k_ends, free, step, low_x, high_x)
    elastic_load(bp, signs, load)

    def first_pass(i, carry):
        for j in range(free.shape[1]):
            disp[i + 1, j + 1] = step[i, j] * load[i, j]
        return carry

    lax.fori_loop(0, free.shape[0], first_pass, 0)
    for k in range(1, MECH_PASSES):
        elastic_pass(ERIM - k, disp, load, free, step, k_own, k_ends, low_x, high_x, cx)
    elastic_strain(disp, signs, strain)

    def pack(i, carry):
        for j in range(packed.shape[1]):
            d = disp[i + ERIM, j + ERIM]
            packed[i, j] = jnp.where(tile_row()[:, :128] < 4, d[:, :128], pltpu.roll(d[:, 128:], 4, 0))
        return carry

    lax.fori_loop(0, packed.shape[0], pack, 0)


def second_flow(
    fp, fs, ends, place, p_own, s_own, d_ext, d_own, k_own, k_ends, signs,
    base, stress, biot, tx, ty, ty_low, tz, tz_low, inv_den, free, step,
    out, strain_out, start, spare, num, strain, bp, disp, load, low_x, high_x,
):
    ex = start.shape[0]
    cx, cy = p_own.shape[0], p_own.shape[1]

    def gather(x, carry):
        apart = jnp.dot(ends[x], place[...], preferred_element_type=F32)
        start[x] = jnp.concatenate([fp[x].astype(F32), apart[:, :128]], axis=1)
        strain[x] = jnp.concatenate([fs[x].astype(F32), apart[:, 128:]], axis=1)
        return carry

    lax.fori_loop(0, ex, gather, 0, unroll=2)
    start[RIM : RIM + cx, RIM : RIM + cy, :] = p_own[...]
    strain[RIM : RIM + cx, RIM : RIM + cy, :] = s_own[...]

    def numerator(x, carry):
        num[x] = base[x] + stress[x] * start[x] - biot[x] * strain[x]
        return carry

    lax.fori_loop(2, ex - 2, numerator, 0, unroll=2)
    flow_passes(start, spare, num, tx, ty, ty_low, tz, tz_low, inv_den, biot, bp, out)
    elastic_load(bp, signs, load)

    def unpacked(d):
        wide = jnp.concatenate([d, pltpu.roll(d, 4, 0)], axis=1)
        return jnp.where(tile_row() < 4, wide, pltpu.roll(roll_up(wide, 1), 4, 0))

    def unpack(i, carry):
        for j in range(d_ext.shape[1]):
            disp[i, j] = unpacked(d_ext[i, j].astype(F32))
        return carry

    lax.fori_loop(0, d_ext.shape[0], unpack, 0)

    def unpack_own(i, carry):
        for j in range(d_own.shape[1]):
            disp[i + ERIM, j + ERIM] = unpacked(d_own[i, j])
        return carry

    lax.fori_loop(0, d_own.shape[0], unpack_own, 0)
    for k in range(MECH_PASSES):
        elastic_pass(ERIM - k, disp, load, free, step, k_own, k_ends, low_x, high_x, cx)
    elastic_strain(disp, signs, strain_out)


def vmem(n):
    return [pl.BlockSpec(memory_space=pltpu.VMEM)] * n


def end_places(count, width, fields):
    place = np.zeros((128, 128 * count), np.float32)
    for i in range(count):
        after, ahead = fields(i)
        for t in range(width):
            place[after + t, 128 * i + t] = 1.0
            place[ahead + t, 128 * i + 128 - width + t] = 1.0
    return jnp.asarray(place, BF)


def per_device(
    pressure_start,
    saturation,
    permeability,
    rock_type,
    rock_table,
    well_cells,
    well_rates,
    owner_map,
    stiffness,
    anchored,
):
    cx, cy, cz = pressure_start.shape
    count_x = lax.axis_size(GX)
    total_x = cx * count_x
    total_y = cy * lax.axis_size("gy")
    total_z = cz * lax.axis_size("grp")
    start_x = lax.axis_index(GX) * cx
    start_y = lax.axis_index("gy") * cy
    start_z = lax.axis_index("grp") * cz
    order, sign = row_order()
    ex, ey = cx + 2 * RIM, cy + 2 * RIM

    owners = owner_map.reshape(-1)
    capacity = stiffness.shape[4]
    one_hot = (owners[:, None] == jnp.arange(count_x, dtype=jnp.int32)[None, :]).astype(jnp.int32)
    before = jnp.cumsum(one_hot, axis=0) - one_hot
    brick_rank = jnp.sum(before * one_hot, axis=1)
    lanes_of = np.zeros((4, 24, 128), np.float32)
    for j in range(4):
        lanes_of[j, :, 32 * j : 32 * j + 32] = order.T
    lanes_of = jnp.asarray(lanes_of, BF)
    held_blocks = stiffness.reshape(count_x, capacity // 4, 4, 24, 24)
    packed = sum(
        jnp.einsum("ogrk,km->ogrm", held_blocks[:, :, j], lanes_of[j], preferred_element_type=F32) for j in range(4)
    ).astype(BF)
    fetched = core_and_chips(packed, (("gx_0", "gx_1"), "gx_2"), (1, 0), 0, 0)
    groups = fetched.reshape(count_x * (capacity // 4), 24, 128)[owners * (capacity // 4) + brick_rank // 4]
    lane_at = lax.broadcasted_iota(jnp.int32, groups.shape, 2) // 32
    groups = jnp.where(lane_at == (brick_rank % 4)[:, None, None], groups, 0)
    fold = jnp.asarray(np.tile(np.eye(32, dtype=np.float32), (4, 1)), BF)
    half = jnp.einsum("brm,mc->brc", groups, fold, preferred_element_type=F32).astype(BF)
    block = jnp.einsum("ar,brc->bac", jnp.asarray(order, BF), half, preferred_element_type=F32).astype(BF)
    block = block.reshape(cx, cy, 32, 32)

    exponents = pick(rock_type, rock_table[:2])
    mobility = jnp.exp(exponents[0] * jnp.log(saturation)) + 2.0 * jnp.exp(
        exponents[1] * jnp.log(1.0 - saturation)
    )
    conductance = permeability * mobility
    fields = [a.astype(BF) for a in (pressure_start, conductance, rock_type, anchored)]

    def k_lanes(b):
        return lane_pad(jnp.concatenate([b[:, i] for i in range(ERIM)], axis=-1))

    got = exchange(
        rows_of(*fields, k_lanes(block[:, :ERIM])),
        rows_of(*fields, k_lanes(block[:, cy - ERIM :])),
        "gy",
        False,
    )
    shapes = [(cx, cy, cz)] * 4 + [(cx, 32, 128)]
    low, high = cut_rows(got[0], shapes), cut_rows(got[1], shapes)
    fields = [jnp.concatenate([low[i], fields[i], high[i]], axis=1) for i in range(4)]

    def k_apart(lanes):
        return jnp.stack([lanes[:, :, 32 * i : 32 * i + 32] for i in range(ERIM)], axis=1)

    block = jnp.concatenate([k_apart(low[4]), block, k_apart(high[4])], axis=1)
    ky = cy + 2 * ERIM

    quad = block.reshape(2, 4, ky, 32, 32)
    quad = jnp.concatenate([quad[:, i] for i in range(4)], axis=-1)
    got = exchange(
        rows_of(lane_pad(jnp.concatenate([f[..., :ZRIM] for f in fields], axis=-1)), quad),
        rows_of(lane_pad(jnp.concatenate([f[..., cz - ZRIM :] for f in fields], axis=-1)), quad),
        "grp",
        False,
    )
    shapes = [(cx, ey, 128), (2, ky, 32, 128)]
    low, high = cut_rows(got[0], shapes), cut_rows(got[1], shapes)
    ends = lane_pad(jnp.concatenate([high[0][..., : 4 * ZRIM], low[0][..., : 4 * ZRIM]], axis=-1))

    def quad_apart(q):
        return jnp.stack([q[..., 32 * i : 32 * i + 32] for i in range(4)], axis=1).reshape(cx, ky, 32, 32)

    after, ahead = quad_apart(high[1]), quad_apart(low[1])

    def k_three(cut):
        return lane_pad(jnp.concatenate([block[cut], after[cut], ahead[cut]], axis=-1))

    got = exchange(
        rows_of(*fields, ends, k_three(slice(0, ERIM))),
        rows_of(*fields, ends, k_three(slice(cx - ERIM, cx))),
        GX,
        True,
    )
    shapes = [(cx, ey, 128)] * 5 + [(ERIM, ky, 32, 128)]
    low, high = cut_rows(got[0], shapes), cut_rows(got[1], shapes)
    fields = [jnp.concatenate([low[i], fields[i], high[i]], axis=0) for i in range(4)]
    ends = jnp.concatenate([low[4], ends, high[4]], axis=0)
    k_own = jnp.concatenate([low[5][..., :32], block, high[5][..., :32]], axis=0)
    k_ends = jnp.concatenate(
        [
            jnp.concatenate([low[5][..., 32:64], after, high[5][..., 32:64]], axis=0),
            jnp.concatenate([low[5][..., 64:96], ahead, high[5][..., 64:96]], axis=0),
        ],
        axis=2,
    )

    plane = total_y * total_z
    well_x = (well_cells // plane - start_x + RIM) % total_x
    well_y = well_cells // total_z % total_y - start_y + RIM
    well_z = well_cells % total_z - start_z
    near = (well_z >= -ZRIM) & (well_z < cz + ZRIM)
    lane = jnp.where(near, well_z % 256, -1)
    at_x = (jnp.arange(ex, dtype=jnp.int32)[:, None] == well_x[None, :]).astype(F32)
    at_y = (jnp.arange(ey, dtype=jnp.int32)[:, None] == well_y[None, :]).astype(F32)
    at_xy = (at_x[:, None, :] * at_y[None, :, :]).reshape(ex * ey, -1)
    at_z = jnp.where(lane[:, None] == jnp.arange(256, dtype=jnp.int32)[None, :], well_rates[:, None], 0.0)
    source = jnp.dot(at_xy, at_z, precision=lax.Precision.HIGHEST).reshape(ex, ey, 256)
    cells = jax.ShapeDtypeStruct((ex, ey, 256), F32)
    tall = jax.ShapeDtypeStruct((cx, cy, 256), F32)
    n = cx + 2 * ERIM
    node = jax.ShapeDtypeStruct((n - 1, n - 1, 8, 256), F32)
    buf = pltpu.VMEM((ex, ey, 256), F32)
    bp_buf = pltpu.VMEM((n, ey, 256), F32)
    elastic_bufs = [
        pltpu.VMEM((n + 1, n + 1, 8, 256), F32),
        pltpu.VMEM((n - 1, n - 1, 8, 256), F32),
        pltpu.VMEM((n, n - 1, 8, 256), F32),
        pltpu.VMEM((n, n - 1, 8, 256), F32),
    ]
    signs = jnp.asarray(np.broadcast_to(sign.reshape(4, 8, 1), (4, 8, 256)), F32)
    z_range = jnp.stack([start_z, jnp.int32(total_z)]).astype(jnp.int32)
    p1, s1, d_pack, *static = pl.pallas_call(
        first_flow,
        out_shape=[tall, tall, jax.ShapeDtypeStruct((cx + 1, cy + 1, 8, 128), F32)] + [cells] * 9 + [node] * 2,
        in_specs=[pl.BlockSpec(memory_space=pltpu.SMEM)] * 2 + vmem(12),
        out_specs=vmem(14),
        scratch_shapes=[buf] * 5 + [bp_buf] + elastic_bufs,
        name="first_iteration",
    )(
        rock_table, z_range, *fields, ends, end_places(4, ZRIM, lambda i: (i * ZRIM, (4 + i) * ZRIM)),
        pressure_start, conductance, source, k_own, k_ends, signs,
    )

    def ends_of(a):
        return jnp.concatenate([a[..., 128 : 128 + ZR1], a[..., 256 - ZR1 :]], axis=-1)

    p_bf, s_bf = p1.astype(BF), s1.astype(BF)
    moving = [p_bf[..., :128], s_bf[..., :128], lane_pad(jnp.concatenate([ends_of(p_bf), ends_of(s_bf)], axis=-1))]
    d_bf = d_pack.astype(BF)
    got = exchange(
        rows_of(*moving, d_bf[:, 1 : 1 + ERIM]),
        rows_of(*moving, d_bf[:, cy - ERIM : cy]),
        "gy",
        False,
    )
    shapes = [(cx, cy, 128)] * 3 + [(cx + 1, ERIM, 8, 128)]
    low, high = cut_rows(got[0], shapes), cut_rows(got[1], shapes)
    moving = [jnp.concatenate([low[i], moving[i], high[i]], axis=1) for i in range(3)]
    d_bf = jnp.concatenate([low[3], d_bf, high[3]], axis=1)
    got = exchange(
        rows_of(*moving, d_bf[1 : 1 + ERIM]),
        rows_of(*moving, d_bf[cx - ERIM : cx]),
        GX,
        True,
    )
    shapes = [(cx, ey, 128)] * 3 + [(ERIM, cy + 1 + 2 * ERIM, 8, 128)]
    low, high = cut_rows(got[0], shapes), cut_rows(got[1], shapes)
    moving = [jnp.concatenate([low[i], moving[i], high[i]], axis=0) for i in range(3)]
    d_bf = jnp.concatenate([low[3], d_bf, high[3]], axis=0)
    short = jax.ShapeDtypeStruct((cx, cy, cz), F32)
    return pl.pallas_call(
        second_flow,
        out_shape=[short, short],
        in_specs=vmem(11 + 11),
        out_specs=vmem(2),
        scratch_shapes=[buf] * 4 + [bp_buf] + elastic_bufs,
        name="second_iteration",
    )(
        *moving, end_places(2, ZR1, lambda i: (2 * i * ZR1, (2 * i + 1) * ZR1)), p1, s1,
        d_bf, d_pack, k_own, k_ends, signs, *static,
    )


def solution(mesh):
    torus = Mesh(
        mesh.devices.reshape(mesh.shape["grp"], 4, 2, 2, mesh.shape["gy"]),
        ("grp", "gx_0", "gx_1", "gx_2", "gy"),
    )
    return jax.shard_map(
        per_device,
        mesh=torus,
        in_specs=(
            P(GX, "gy", "grp"),
            P(GX, "gy", "grp"),
            P(GX, "gy", "grp"),
            P(GX, "gy", "grp"),
            P(),
            P(),
            P(),
            P(GX, "gy", "grp", None, None),
            P(GX, "gy", "grp", None, None, None, None),
            P(GX, "gy", "grp"),
        ),
        out_specs=(P(GX, "gy", "grp"), P(GX, "gy", "grp")),
        check_vma=False,
    )
```

profile of v0, /device:TPU:2, one launch (start us, length us, event | category | flops | bytes accessed | tf_op | source)
XLA Modules:
  0.0 166.2 jit_solution(2914016515104134093)
XLA Ops:
  0.7 1.2 fusion.20
  4.2 1.1 fusion
  5.4 3.9 %all_to_all.10 = bf16[8,2,1,2,24,128]{5,4,3,0,2,1:T(8,128)(2,1)S(1)} all-to-all(bf16[8,2,1,2,24,128]{5,4,3,0,2,1:T(8,128)(2,1)S(1)} %copy.81), channel_id=1, replica_groups=mesh['grp'=4,'gx_0'=4,'gx_1'=2,'gx_2'=2,'gy'=4] {'gx_2'}, dimensions={1} | all-to-all | bytes 393216 | tf_op jit(solution)/shard_map/all_to_all | solution.py:76
  10.0 5.8 %all-to-all-start.1 = ((bf16[8,2,1,2,24,128]{5,4,3,1,2,0:T(8,128)(2,1)}), bf16[8,2,1,2,24,128]{5,4,3,1,2,0:T(8,128)(2,1)S(1)}, u32[]{:S(2)}, u32[]{:S(2)}) async-start(bf16[8,2,1,2,24,128]{5,4,3,1,2,0:T(8,128)(2,1)} %copy.82), calls=%async_computation.1 | async-start | bytes 393216 | tf_op jit(solution)/shard_map/all_to_all | solution.py:76
  17.4 5.3 %all-to-all-done.1 = bf16[8,2,1,2,24,128]{5,4,3,1,2,0:T(8,128)(2,1)S(1)} async-done(((bf16[8,2,1,2,24,128]{5,4,3,1,2,0:T(8,128)(2,1)}), bf16[8,2,1,2,24,128]{5,4,3,1,2,0:T(8,128)(2,1)S(1)}, u32[]{:S(2)}, u32[]{:S(2)}) %all-to-all-start.1) | async-done | bytes 196640 | tf_op jit(solution)/shard_map/all_to_all | solution.py:76
  25.5 5.2 %collective-permute-start = (bf16[512,128]{1,0:T(8,128)(2,1)S(1)}, bf16[512,128]{1,0:T(8,128)(2,1)S(1)}, u32[]{:S(2)}, u32[]{:S(2)}) collective-permute-start(bf16[512,128]{1,0:T(8,128)(2,1)S(1)} %constant_dynamic-update-slice_fusion), channel_id=1, source_target_pairs={{0,1},{1,2},{2,3},{4,5},{5,6},{6,7},{8,9},{9,10},{10,11},{12,13},{... | collective-permute-start | bytes 393224 | tf_op jit(solution)/shard_map/ppermute | solution.py:40
  30.8 1.3 collective-permute-start.1
  33.3 8.2 %collective-permute-done.1 = bf16[512,128]{1,0:T(8,128)(2,1)S(1)} collective-permute-done((bf16[512,128]{1,0:T(8,128)(2,1)S(1)}, bf16[512,128]{1,0:T(8,128)(2,1)S(1)}, u32[]{:S(2)}, u32[]{:S(2)}) %collective-permute-start.1) | collective-permute-done | bytes 131104 | tf_op jit(solution)/shard_map/ppermute | solution.py:40
  42.9 3.4 %collective-permute-start.3 = (bf16[1088,128]{1,0:T(8,128)(2,1)S(1)}, bf16[1088,128]{1,0:T(8,128)(2,1)S(1)}, u32[]{:S(2)}, u32[]{:S(2)}) collective-permute-start(bf16[1088,128]{1,0:T(8,128)(2,1)S(1)} %pad_maximum_fusion.6), channel_id=1, source_target_pairs={{0,64},{64,128},{128,192},{1,65},{65,129},{129,193},{2,66},{66,130... | collective-permute-start | bytes 835592 | tf_op jit(solution)/shard_map/ppermute | solution.py:40
  46.3 2.5 %collective-permute-start.2 = (bf16[1088,128]{1,0:T(8,128)(2,1)S(1)}, bf16[1088,128]{1,0:T(8,128)(2,1)S(1)}, u32[]{:S(2)}, u32[]{:S(2)}) collective-permute-start(bf16[1088,128]{1,0:T(8,128)(2,1)S(1)} %get-tuple-element.30), channel_id=1, source_target_pairs={{64,0},{128,64},{192,128},{65,1},{129,65},{193,129},{66,2},{130,66... | collective-permute-start | bytes 835592 | tf_op jit(solution)/shard_map/ppermute | solution.py:40
  49.4 3.5 %collective-permute-done.3 = bf16[1088,128]{1,0:T(8,128)(2,1)S(1)} collective-permute-done((bf16[1088,128]{1,0:T(8,128)(2,1)S(1)}, bf16[1088,128]{1,0:T(8,128)(2,1)S(1)}, u32[]{:S(2)}, u32[]{:S(2)}) %collective-permute-start.3) | collective-permute-done | bytes 278560 | tf_op jit(solution)/shard_map/ppermute | solution.py:40
  52.9 3.1 %collective-permute-done.2 = bf16[1088,128]{1,0:T(8,128)(2,1)S(1)} collective-permute-done((bf16[1088,128]{1,0:T(8,128)(2,1)S(1)}, bf16[1088,128]{1,0:T(8,128)(2,1)S(1)}, u32[]{:S(2)}, u32[]{:S(2)}) %collective-permute-start.2) | collective-permute-done | bytes 278560 | tf_op jit(solution)/shard_map/ppermute | solution.py:40
  58.4 4.1 %collective-permute-start.5 = (bf16[2304,128]{1,0:T(8,128)(2,1)S(1)}, bf16[2304,128]{1,0:T(8,128)(2,1)S(1)}, u32[]{:S(2)}, u32[]{:S(2)}) collective-permute-start(bf16[2304,128]{1,0:T(8,128)(2,1)S(1)} %constant_dynamic-update-slice_fusion.30), channel_id=1, source_target_pairs={{4,0},{8,4},{12,8},{16,12},{20,16},{24,20},{28,24},{32,28},{36,32}... | collective-permute-start | bytes 1769480 | tf_op jit(solution)/shard_map/ppermute | solution.py:40
  63.1 1.5 fusion.18.source
  64.6 8.4 %collective-permute-done.4 = bf16[2304,128]{1,0:T(8,128)(2,1)S(1)} collective-permute-done((bf16[2304,128]{1,0:T(8,128)(2,1)S(1)}, bf16[2304,128]{1,0:T(8,128)(2,1)S(1)}, u32[]{:S(2)}, u32[]{:S(2)}) %collective-permute-start.4) | collective-permute-done | bytes 589856 | tf_op jit(solution)/shard_map/ppermute | solution.py:40
  77.0 1.5 pad_maximum_fusion.k_own
  78.6 2.2 %maximum_maximum_fusion.k_ends = bf16[14,14,64,32]{3,2,1,0:T(8,128)(2,1)} fusion(bf16[3,14,32,32]{3,2,1,0:T(8,128)(2,1)S(1)} %get-tuple-element.71, bf16[8,14,32,32]{3,2,1,0:T(8,128)(2,1)S(1)} %bitcast.290, bf16[3,14,32,32]{3,2,1,0:T(8,128)(2,1)S(1)} %get-tuple-element.68, bf16[3,14,32,32]{3,2,1,0:T(8,128)(2,1)S(1)} %get-tuple-element.70, ...), kind=kLoop, calls=%fused_computation.1 | loop fusion | flops 4816896 | bytes 1605632 | tf_op jit(solution)/shard_map/concatenate | solution.py:493
  81.4 28.8 %first_iteration.1 = (f32[8,8,256]{2,1,0:T(8,128)}, f32[8,8,256]{2,1,0:T(8,128)}, f32[9,9,8,128]{3,2,1,0:T(8,128)}, f32[24,24,256]{2,1,0:T(8,128)}, f32[24,24,25...) custom-call(f32[5,4]{1,0:T(8,128)} %copy-done.5, ...), custom_call_target="tpu_custom_call" | custom-call | tf_op jit(solution)/shard_map/first_iteration/pallas_call | solution.py:526
  113.3 6.9 %collective-permute-start.6 = (bf16[408,128]{1,0:T(8,128)(2,1)S(1)}, bf16[408,128]{1,0:T(8,128)(2,1)S(1)}, u32[]{:S(2)}, u32[]{:S(2)}) collective-permute-start(bf16[408,128]{1,0:T(8,128)(2,1)S(1)} %get-tuple-element.113), channel_id=1, source_target_pairs={{0,1},{1,2},{2,3},{4,5},{5,6},{6,7},{8,9},{9,10},{10,11},{12,13},{... | collective-permute-start | bytes 313352 | tf_op jit(solution)/shard_map/ppermute | solution.py:40
  120.1 1.3 collective-permute-start.7
  122.4 5.2 %collective-permute-done.7 = bf16[408,128]{1,0:T(8,128)(2,1)S(1)} collective-permute-done((bf16[408,128]{1,0:T(8,128)(2,1)S(1)}, bf16[408,128]{1,0:T(8,128)(2,1)S(1)}, u32[]{:S(2)}, u32[]{:S(2)}) %collective-permute-start.7) | collective-permute-done | bytes 104480 | tf_op jit(solution)/shard_map/ppermute | solution.py:40
  127.8 3.8 %collective-permute-start.9 = (bf16[936,128]{1,0:T(8,128)(2,1)S(1)}, bf16[936,128]{1,0:T(8,128)(2,1)S(1)}, u32[]{:S(2)}, u32[]{:S(2)}) collective-permute-start(bf16[936,128]{1,0:T(8,128)(2,1)S(1)} %get-tuple-element.92), channel_id=1, source_target_pairs={{4,0},{8,4},{12,8},{16,12},{20,16},{24,20},{28,24},{32,28},{36,32}... | collective-permute-start | bytes 718856 | tf_op jit(solution)/shard_map/ppermute | solution.py:40
  131.7 4.3 %collective-permute-done.8 = bf16[936,128]{1,0:T(8,128)(2,1)S(1)} collective-permute-done((bf16[936,128]{1,0:T(8,128)(2,1)S(1)}, bf16[936,128]{1,0:T(8,128)(2,1)S(1)}, u32[]{:S(2)}, u32[]{:S(2)}) %collective-permute-start.8) | collective-permute-done | bytes 239648 | tf_op jit(solution)/shard_map/ppermute | solution.py:40
  138.9 27.3 %second_iteration.1 = (f32[8,8,128]{2,1,0:T(8,128)}, f32[8,8,128]{2,1,0:T(8,128)}) custom-call(bf16[24,24,128]{2,1,0:T(8,128)(2,1)} %pad_maximum_fusion.15.fp, bf16[24,24,128]{2,1,0:T(8,128)(2,1)} %pad_maximum_fusion.16.fs, bf16[24,24,128]{2,1,0:T(8,128)(2,1)} %pad_maximum_fusion.17.ends, bf16[128,256]{1,0:T(8,128)(2,1)} %constant.171.clone.place, ...), custom_call_target="tpu_custom_call" | custom-call | tf_op jit(solution)/shard_map/second_iteration/pallas_call | solution.py:565
  (159 shorter events, 24.9 us)
Async XLA Ops:
  0.6 15.2 %copy-start.7 = (s32[1,1,1,64,1]{3,4,2,1,0:T(1,128)S(1)}, s32[1,1,1,64,1]{3,4,2,1,0:T(1,128)}, u32[]{:S(2)}) copy-start(s32[1,1,1,64,1]{3,4,2,1,0:T(1,128)} %param.23) | copy-start | bytes 772
  0.6 15.6 %copy-start.8 = (f32[5,4]{0,1:T(4,128)S(1)}, f32[5,4]{0,1:T(4,128)}, u32[]{:S(2)}) copy-start(f32[5,4]{0,1:T(4,128)} %param.20) | copy-start | bytes 244
  0.7 15.6 %copy-start.1 = (s32[8,8,128]{2,1,0:T(8,128)S(1)}, s32[8,8,128]{2,1,0:T(8,128)}, u32[]{:S(2)}) copy-start(s32[8,8,128]{2,1,0:T(8,128)} %param.19) | copy-start | bytes 98308
  0.7 15.9 %copy-start = (f32[8,8,128]{2,1,0:T(8,128)S(1)}, f32[8,8,128]{2,1,0:T(8,128)}, u32[]{:S(2)}) copy-start(f32[8,8,128]{2,1,0:T(8,128)} %p_own.1) | copy-start | bytes 98308
  0.7 15.9 %copy-start.3 = (f32[8,8,128]{2,1,0:T(8,128)S(1)}, f32[8,8,128]{2,1,0:T(8,128)}, u32[]{:S(2)}) copy-start(f32[8,8,128]{2,1,0:T(8,128)} %param.18) | copy-start | bytes 98308
  0.7 15.9 %copy-start.4 = (f32[8,8,128]{2,1,0:T(8,128)S(1)}, f32[8,8,128]{2,1,0:T(8,128)}, u32[]{:S(2)}) copy-start(f32[8,8,128]{2,1,0:T(8,128)} %param.17) | copy-start | bytes 98308
  0.7 16.6 %copy-start.2 = (s32[8,8,128]{2,1,0:T(8,128)S(1)}, s32[8,8,128]{2,1,0:T(8,128)}, u32[]{:S(2)}) copy-start(s32[8,8,128]{2,1,0:T(8,128)} %param.25) | copy-start | bytes 98308
  0.7 16.6 %copy-start.11 = (s32[64]{0:T(128)S(1)}, s32[64]{0:T(128)}, u32[]{:S(2)}) copy-start(s32[64]{0:T(128)} %param.21) | copy-start | bytes 772
  1.9 21.5 %copy-start.12 = (bf16[128,32,1]{0,1,2:T(8,128)(2,1)S(1)}, bf16[128,32,1]{0,1,2:T(8,128)(2,1)}, u32[]{:S(2)}) copy-start(bf16[128,32,1]{0,1,2:T(8,128)(2,1)} %constant.207) | copy-start | bytes 24580
  4.2 19.9 %copy-start.6 = (bf16[32,24,1]{0,1,2:T(8,128)(2,1)S(1)}, bf16[32,24,1]{0,1,2:T(8,128)(2,1)}, u32[]{:S(2)}) copy-start(bf16[32,24,1]{0,1,2:T(8,128)(2,1)} %constant.208) | copy-start | bytes 4612
  10.0 12.8 %all-to-all-start.1 = ((bf16[8,2,1,2,24,128]{5,4,3,1,2,0:T(8,128)(2,1)}), bf16[8,2,1,2,24,128]{5,4,3,1,2,0:T(8,128)(2,1)S(1)}, u32[]{:S(2)}, u32[]{:S(2)}) async-start(bf16[8,2,1,2,24,128]{5,4,3,1,2,0:T(8,128)(2,1)} %copy.82), calls=%async_computation.1 | async-start | bytes 393216 | tf_op jit(solution)/shard_map/all_to_all | solution.py:76
  16.3 14.5 %copy-start.5 = (f32[5,4]{1,0:T(8,128)}, f32[5,4]{1,0:T(8,128)S(1)}, u32[]{:S(2)}) copy-start(f32[5,4]{1,0:T(8,128)S(1)} %copy.106.table) | copy-start | bytes 244
  25.5 7.7 %collective-permute-start = (bf16[512,128]{1,0:T(8,128)(2,1)S(1)}, bf16[512,128]{1,0:T(8,128)(2,1)S(1)}, u32[]{:S(2)}, u32[]{:S(2)}) collective-permute-start(bf16[512,128]{1,0:T(8,128)(2,1)S(1)} %constant_dynamic-update-slice_fusion), channel_id=1, source_target_pairs={{0,1},{1,2},{2,3},{4,5},{5,6},{6,7},{8,9},{9,10},{10,11},{12,13},{... | collective-permute-start | bytes 393224 | tf_op jit(solution)/shard_map/ppermute | solution.py:40
  30.8 10.7 %collective-permute-start.1 = (bf16[512,128]{1,0:T(8,128)(2,1)S(1)}, bf16[512,128]{1,0:T(8,128)(2,1)S(1)}, u32[]{:S(2)}, u32[]{:S(2)}) collective-permute-start(bf16[512,128]{1,0:T(8,128)(2,1)S(1)} %constant_dynamic-update-slice_fusion.5), channel_id=1, source_target_pairs={{1,0},{2,1},{3,2},{5,4},{6,5},{7,6},{9,8},{10,9},{11,10},{13,12},{... | collective-permute-start | bytes 393224 | tf_op jit(solution)/shard_map/ppermute | solution.py:40
  42.9 10.0 %collective-permute-start.3 = (bf16[1088,128]{1,0:T(8,128)(2,1)S(1)}, bf16[1088,128]{1,0:T(8,128)(2,1)S(1)}, u32[]{:S(2)}, u32[]{:S(2)}) collective-permute-start(bf16[1088,128]{1,0:T(8,128)(2,1)S(1)} %pad_maximum_fusion.6), channel_id=1, source_target_pairs={{0,64},{64,128},{128,192},{1,65},{65,129},{129,193},{2,66},{66,130... | collective-permute-start | bytes 835592 | tf_op jit(solution)/shard_map/ppermute | solution.py:40
  46.3 9.7 %collective-permute-start.2 = (bf16[1088,128]{1,0:T(8,128)(2,1)S(1)}, bf16[1088,128]{1,0:T(8,128)(2,1)S(1)}, u32[]{:S(2)}, u32[]{:S(2)}) collective-permute-start(bf16[1088,128]{1,0:T(8,128)(2,1)S(1)} %get-tuple-element.30), channel_id=1, source_target_pairs={{64,0},{128,64},{192,128},{65,1},{129,65},{193,129},{66,2},{130,66... | collective-permute-start | bytes 835592 | tf_op jit(solution)/shard_map/ppermute | solution.py:40
  57.3 5.8 %copy-start.10 = (f32[64]{0:T(128)S(1)}, f32[64]{0:T(128)}, u32[]{:S(2)}) copy-start(f32[64]{0:T(128)} %param.22) | copy-start | bytes 772
  57.8 15.2 %collective-permute-start.4 = (bf16[2304,128]{1,0:T(8,128)(2,1)S(1)}, bf16[2304,128]{1,0:T(8,128)(2,1)S(1)}, u32[]{:S(2)}, u32[]{:S(2)}) collective-permute-start(bf16[2304,128]{1,0:T(8,128)(2,1)S(1)} %constant_dynamic-update-slice_fusion.24), channel_id=1, source_target_pairs={{0,4},{4,8},{8,12},{12,16},{16,20},{20,24},{24,28},{28,32},{32,36}... | collective-permute-start | bytes 1769480 | tf_op jit(solution)/shard_map/ppermute | solution.py:40
  58.4 15.0 %collective-permute-start.5 = (bf16[2304,128]{1,0:T(8,128)(2,1)S(1)}, bf16[2304,128]{1,0:T(8,128)(2,1)S(1)}, u32[]{:S(2)}, u32[]{:S(2)}) collective-permute-start(bf16[2304,128]{1,0:T(8,128)(2,1)S(1)} %constant_dynamic-update-slice_fusion.30), channel_id=1, source_target_pairs={{4,0},{8,4},{12,8},{16,12},{20,16},{24,20},{28,24},{32,28},{36,32}... | collective-permute-start | bytes 1769480 | tf_op jit(solution)/shard_map/ppermute | solution.py:40
  78.6 2.2 %copy-start.9 = (f32[4,8]{1,0:T(4,128)S(1)}, f32[4,8]{1,0:T(4,128)}, u32[]{:S(2)}) copy-start(f32[4,8]{1,0:T(4,128)} %constant.169.clone) | copy-start | bytes 388
  113.3 9.1 %collective-permute-start.6 = (bf16[408,128]{1,0:T(8,128)(2,1)S(1)}, bf16[408,128]{1,0:T(8,128)(2,1)S(1)}, u32[]{:S(2)}, u32[]{:S(2)}) collective-permute-start(bf16[408,128]{1,0:T(8,128)(2,1)S(1)} %get-tuple-element.113), channel_id=1, source_target_pairs={{0,1},{1,2},{2,3},{4,5},{5,6},{6,7},{8,9},{9,10},{10,11},{12,13},{... | collective-permute-start | bytes 313352 | tf_op jit(solution)/shard_map/ppermute | solution.py:40
  120.1 7.5 %collective-permute-start.7 = (bf16[408,128]{1,0:T(8,128)(2,1)S(1)}, bf16[408,128]{1,0:T(8,128)(2,1)S(1)}, u32[]{:S(2)}, u32[]{:S(2)}) collective-permute-start(bf16[408,128]{1,0:T(8,128)(2,1)S(1)} %get-tuple-element.114), channel_id=1, source_target_pairs={{1,0},{2,1},{3,2},{5,4},{6,5},{7,6},{9,8},{10,9},{11,10},{13,12},{... | collective-permute-start | bytes 313352 | tf_op jit(solution)/shard_map/ppermute | solution.py:40
  127.7 8.3 %collective-permute-start.8 = (bf16[936,128]{1,0:T(8,128)(2,1)S(1)}, bf16[936,128]{1,0:T(8,128)(2,1)S(1)}, u32[]{:S(2)}, u32[]{:S(2)}) collective-permute-start(bf16[936,128]{1,0:T(8,128)(2,1)S(1)} %get-tuple-element.91), channel_id=1, source_target_pairs={{0,4},{4,8},{8,12},{12,16},{16,20},{20,24},{24,28},{28,32},{32,36}... | collective-permute-start | bytes 718856 | tf_op jit(solution)/shard_map/ppermute | solution.py:40
  127.8 8.2 %collective-permute-start.9 = (bf16[936,128]{1,0:T(8,128)(2,1)S(1)}, bf16[936,128]{1,0:T(8,128)(2,1)S(1)}, u32[]{:S(2)}, u32[]{:S(2)}) collective-permute-start(bf16[936,128]{1,0:T(8,128)(2,1)S(1)} %get-tuple-element.92), channel_id=1, source_target_pairs={{4,0},{8,4},{12,8},{16,12},{20,16},{24,20},{28,24},{32,28},{36,32}... | collective-permute-start | bytes 718856 | tf_op jit(solution)/shard_map/ppermute | solution.py:40
where the time goes:
time: 167 us; the launch traced here: 166 us
  Pallas kernels  56.1 us (34%)
  waiting for transfers between devices  40.1 us (24%)
  starting transfers between devices  34.4 us (21%)
  other arithmetic  16.8 us (10%)
  matrix products  7.02 us (4%)
  local copies, waits for them, and re-layouts  6.46 us (4%)
  blocking collectives  3.89 us (2%)
    ppermute x10, waiting for transfers between devices, exchange(): return (lax.ppermute(to_high, axis, up), lax.ppermute(to_low, axis, down))  34.7 us
    pallas_call x1, Pallas kernels, per_device(): pl.pallas_call(first_flow, out_shape=[tall, tall, jax.ShapeDtypeStruct((c...  28.8 us
    ppermute x10, starting transfers between devices, exchange(): return (lax.ppermute(to_high, axis, up), lax.ppermute(to_low, axis, down))  28.6 us
    pallas_call x1, Pallas kernels, per_device(): pl.pallas_call(second_flow, out_shape=[short, short], in_specs=vmem(11 +...  27.3 us
    all_to_all x1, starting transfers between devices, exchange_in_order(): lax.all_to_all(parts, axes[k], split_axis=k, concat_axis=k, tiled=True)  5.82 us
    all_to_all x1, waiting for transfers between devices, exchange_in_order(): lax.all_to_all(parts, axes[k], split_axis=k, concat_axis=k, tiled=True)  5.33 us
    dot_general x4, matrix products, per_device(): jnp.einsum('ogrk,km->ogrm', held_blocks[:, :, j], lanes_of[j], preferred_...  4.57 us
    all_to_all x1, blocking collectives, exchange_in_order(): lax.all_to_all(parts, axes[k], split_axis=k, concat_axis=k, tiled=True)  3.89 us
  transfers between devices with their start and end apart: 11, of which 9 were waited for; matrix products, arithmetic and copies ran while one was open for 3% of the time, Pallas kernels for 0%

commit v1 on v0

--- a/solution.py
+++ b/solution.py
@@ -15,7 +15,8 @@
 BF = jnp.bfloat16
 F32 = jnp.float32
 RIM = 8
-ZRIM = 14
+ZRIM = (13, 13, 13, 13, 10)
+ZSIDE = sum(ZRIM)
 ZR1 = 7
 ERIM = 3
 
@@ -249,7 +250,7 @@
 
 
 def first_flow(
-    table, z_range, fp, fc, fr, fh, ends, place, p_own, c_own, source, k_own, k_ends, signs,
+    table, z_range, below, above, f0, f1, f2, f3, f4, ends, place, p_own, c_own, source, k_own, k_ends, signs,
     out, strain, packed, base, stress, biot, tx, ty, ty_low, tz, tz_low, inv_den, free, step,
     start, spare, cond, num, held, bp, disp, load, low_x, high_x,
 ):
@@ -265,21 +266,29 @@
             value = jnp.where(rock == float(r), table[row, r], value)
         return value
 
-    def gather(x, carry):
-        apart = jnp.dot(ends[x], place[...], preferred_element_type=F32)
-        start[x] = jnp.concatenate([fp[x].astype(F32), apart[:, :128]], axis=1)
-        cond[x] = jnp.concatenate([fc[x].astype(F32), apart[:, 128:256]], axis=1)
-        rock = jnp.concatenate([fr[x].astype(F32), apart[:, 256:384]], axis=1)
-        held[x] = jnp.concatenate([fh[x].astype(F32), apart[:, 384:]], axis=1)
-        storage = choose(rock, 2)
-        strained = choose(rock, 3)
-        base[x] = storage
-        stress[x] = strained
-        biot[x] = jnp.where(z_in, choose(rock, 4), 0.0)
-        inv_den[x] = storage + strained
-        return carry
-
-    lax.fori_loop(0, ex, gather, 0, unroll=2)
+    def gather(plane, offset):
+        def one(i, carry):
+            x = i + offset
+            apart = jnp.dot(plane(5, i), place[...], preferred_element_type=F32)
+            fine = plane(0, i).astype(F32) + plane(1, i).astype(F32)
+            start[x] = jnp.concatenate([fine, apart[:, :128]], axis=1)
+            cond[x] = jnp.concatenate([plane(2, i).astype(F32), apart[:, 128:256]], axis=1)
+            rock = jnp.concatenate([plane(3, i).astype(F32), apart[:, 256:384]], axis=1)
+            held[x] = jnp.concatenate([plane(4, i).astype(F32), apart[:, 384:]], axis=1)
+            storage = choose(rock, 2)
+            strained = choose(rock, 3)
+            base[x] = storage
+            stress[x] = strained
+            biot[x] = jnp.where(z_in, choose(rock, 4), 0.0)
+            inv_den[x] = storage + strained
+            return carry
+
+        lax.fori_loop(0, RIM, one, 0, unroll=2)
+
+    own = (f0, f1, f2, f3, f4, ends)
+    gather(lambda f, i: below[f * RIM + i], 0)
+    gather(lambda f, i: own[f][i], RIM)
+    gather(lambda f, i: above[f * RIM + i], RIM + cx)
     start[RIM : RIM + cx, RIM : RIM + p_own.shape[1], 0:128] = p_own[...]
     cond[RIM : RIM + cx, RIM : RIM + p_own.shape[1], 0:128] = c_own[...]
 
@@ -327,20 +336,28 @@
 
 
 def second_flow(
-    fp, fs, ends, place, p_own, s_own, d_ext, d_own, k_own, k_ends, signs,
+    below, above, f0, f1, f2, ends, place, p_own, s_own, d_ext, d_own, k_own, k_ends, signs,
     base, stress, biot, tx, ty, ty_low, tz, tz_low, inv_den, free, step,
     out, strain_out, start, spare, num, strain, bp, disp, load, low_x, high_x,
 ):
     ex = start.shape[0]
     cx, cy = p_own.shape[0], p_own.shape[1]
 
-    def gather(x, carry):
-        apart = jnp.dot(ends[x], place[...], preferred_element_type=F32)
-        start[x] = jnp.concatenate([fp[x].astype(F32), apart[:, :128]], axis=1)
-        strain[x] = jnp.concatenate([fs[x].astype(F32), apart[:, 128:]], axis=1)
-        return carry
-
-    lax.fori_loop(0, ex, gather, 0, unroll=2)
+    def gather(plane, offset):
+        def one(i, carry):
+            x = i + offset
+            apart = jnp.dot(plane(3, i), place[...], preferred_element_type=F32)
+            fine = plane(0, i).astype(F32) + plane(1, i).astype(F32)
+            start[x] = jnp.concatenate([fine, apart[:, :128]], axis=1)
+            strain[x] = jnp.concatenate([plane(2, i).astype(F32), apart[:, 128:]], axis=1)
+            return carry
+
+        lax.fori_loop(0, RIM, one, 0, unroll=2)
+
+    own = (f0, f1, f2, ends)
+    gather(lambda f, i: below[f * RIM + i], 0)
+    gather(lambda f, i: own[f][i], RIM)
+    gather(lambda f, i: above[f * RIM + i], RIM + cx)
     start[RIM : RIM + cx, RIM : RIM + cy, :] = p_own[...]
     strain[RIM : RIM + cx, RIM : RIM + cy, :] = s_own[...]
 
@@ -378,14 +395,18 @@
     return [pl.BlockSpec(memory_space=pltpu.VMEM)] * n
 
 
-def end_places(count, width, fields):
-    place = np.zeros((128, 128 * count), np.float32)
-    for i in range(count):
-        after, ahead = fields(i)
+def end_places(pieces):
+    place = np.zeros((128, 128 * (1 + max(p[0] for p in pieces))), np.float32)
+    for tile, width, after, ahead in pieces:
         for t in range(width):
-            place[after + t, 128 * i + t] = 1.0
-            place[ahead + t, 128 * i + 128 - width + t] = 1.0
+            place[after + t, 128 * tile + t] = 1.0
+            place[ahead + t, 128 * tile + 128 - width + t] = 1.0
     return jnp.asarray(place, BF)
+
+
+def halves(a):
+    high = lax.reduce_precision(a, 8, 7)
+    return high.astype(BF), (a - high).astype(BF)
 
 
 def per_device(
@@ -438,7 +459,7 @@
         exponents[1] * jnp.log(1.0 - saturation)
     )
     conductance = permeability * mobility
-    fields = [a.astype(BF) for a in (pressure_start, conductance, rock_type, anchored)]
+    fields = [*halves(pressure_start)] + [a.astype(BF) for a in (conductance, rock_type, anchored)]
 
     def k_lanes(b):
         return lane_pad(jnp.concatenate([b[:, i] for i in range(ERIM)], axis=-1))
@@ -449,27 +470,27 @@
         "gy",
         False,
     )
-    shapes = [(cx, cy, cz)] * 4 + [(cx, 32, 128)]
+    shapes = [(cx, cy, cz)] * 5 + [(cx, 32, 128)]
     low, high = cut_rows(got[0], shapes), cut_rows(got[1], shapes)
-    fields = [jnp.concatenate([low[i], fields[i], high[i]], axis=1) for i in range(4)]
+    fields = [jnp.concatenate([low[i], fields[i], high[i]], axis=1) for i in range(5)]
 
     def k_apart(lanes):
         return jnp.stack([lanes[:, :, 32 * i : 32 * i + 32] for i in range(ERIM)], axis=1)
 
-    block = jnp.concatenate([k_apart(low[4]), block, k_apart(high[4])], axis=1)
+    block = jnp.concatenate([k_apart(low[5]), block, k_apart(high[5])], axis=1)
     ky = cy + 2 * ERIM
 
     quad = block.reshape(2, 4, ky, 32, 32)
     quad = jnp.concatenate([quad[:, i] for i in range(4)], axis=-1)
     got = exchange(
-        rows_of(lane_pad(jnp.concatenate([f[..., :ZRIM] for f in fields], axis=-1)), quad),
-        rows_of(lane_pad(jnp.concatenate([f[..., cz - ZRIM :] for f in fields], axis=-1)), quad),
+        rows_of(lane_pad(jnp.concatenate([f[..., :w] for f, w in zip(fields, ZRIM)], axis=-1)), quad),
+        rows_of(lane_pad(jnp.concatenate([f[..., cz - w :] for f, w in zip(fields, ZRIM)], axis=-1)), quad),
         "grp",
         False,
     )
     shapes = [(cx, ey, 128), (2, ky, 32, 128)]
     low, high = cut_rows(got[0], shapes), cut_rows(got[1], shapes)
-    ends = lane_pad(jnp.concatenate([high[0][..., : 4 * ZRIM], low[0][..., : 4 * ZRIM]], axis=-1))
+    ends = lane_pad(jnp.concatenate([high[0][..., :ZSIDE], low[0][..., :ZSIDE]], axis=-1))
 
     def quad_apart(q):
         return jnp.stack([q[..., 32 * i : 32 * i + 32] for i in range(4)], axis=1).reshape(cx, ky, 32, 32)
@@ -485,15 +506,14 @@
         GX,
         True,
     )
-    shapes = [(cx, ey, 128)] * 5 + [(ERIM, ky, 32, 128)]
-    low, high = cut_rows(got[0], shapes), cut_rows(got[1], shapes)
-    fields = [jnp.concatenate([low[i], fields[i], high[i]], axis=0) for i in range(4)]
-    ends = jnp.concatenate([low[4], ends, high[4]], axis=0)
-    k_own = jnp.concatenate([low[5][..., :32], block, high[5][..., :32]], axis=0)
+    planes = (len(fields) + 1) * cx * ey
+    low, high = (cut_rows(g[planes:], [(ERIM, ky, 32, 128)])[0] for g in got)
+    below, above = (g.reshape(-1, ey, 128) for g in got)
+    k_own = jnp.concatenate([low[..., :32], block, high[..., :32]], axis=0)
     k_ends = jnp.concatenate(
         [
-            jnp.concatenate([low[5][..., 32:64], after, high[5][..., 32:64]], axis=0),
-            jnp.concatenate([low[5][..., 64:96], ahead, high[5][..., 64:96]], axis=0),
+            jnp.concatenate([low[..., 32:64], after, high[..., 32:64]], axis=0),
+            jnp.concatenate([low[..., 64:96], ahead, high[..., 64:96]], axis=0),
         ],
         axis=2,
     )
@@ -502,17 +522,17 @@
     well_x = (well_cells // plane - start_x + RIM) % total_x
     well_y = well_cells // total_z % total_y - start_y + RIM
     well_z = well_cells % total_z - start_z
-    near = (well_z >= -ZRIM) & (well_z < cz + ZRIM)
+    near = (well_z >= -ZRIM[0]) & (well_z < cz + ZRIM[0])
     lane = jnp.where(near, well_z % 256, -1)
     at_x = (jnp.arange(ex, dtype=jnp.int32)[:, None] == well_x[None, :]).astype(F32)
     at_y = (jnp.arange(ey, dtype=jnp.int32)[:, None] == well_y[None, :]).astype(F32)
     at_xy = (at_x[:, None, :] * at_y[None, :, :]).reshape(ex * ey, -1)
     at_z = jnp.where(lane[:, None] == jnp.arange(256, dtype=jnp.int32)[None, :], well_rates[:, None], 0.0)
     source = jnp.dot(at_xy, at_z, precision=lax.Precision.HIGHEST).reshape(ex, ey, 256)
-    cells = jax.ShapeDtypeStruct((ex, ey, 256), F32)
-    tall = jax.ShapeDtypeStruct((cx, cy, 256), F32)
+    cells = pltpu.VMEM((ex, ey, 256), F32)
+    tall = pltpu.VMEM((cx, cy, 256), F32)
     n = cx + 2 * ERIM
-    node = jax.ShapeDtypeStruct((n - 1, n - 1, 8, 256), F32)
+    node = pltpu.VMEM((n - 1, n - 1, 8, 256), F32)
     buf = pltpu.VMEM((ex, ey, 256), F32)
     bp_buf = pltpu.VMEM((n, ey, 256), F32)
     elastic_bufs = [
@@ -521,25 +541,27 @@
         pltpu.VMEM((n, n - 1, 8, 256), F32),
         pltpu.VMEM((n, n - 1, 8, 256), F32),
     ]
+    z_pieces = [(max(i - 1, 0), w, sum(ZRIM[:i]), ZSIDE + sum(ZRIM[:i])) for i, w in enumerate(ZRIM)]
     signs = jnp.asarray(np.broadcast_to(sign.reshape(4, 8, 1), (4, 8, 256)), F32)
     z_range = jnp.stack([start_z, jnp.int32(total_z)]).astype(jnp.int32)
     p1, s1, d_pack, *static = pl.pallas_call(
         first_flow,
-        out_shape=[tall, tall, jax.ShapeDtypeStruct((cx + 1, cy + 1, 8, 128), F32)] + [cells] * 9 + [node] * 2,
-        in_specs=[pl.BlockSpec(memory_space=pltpu.SMEM)] * 2 + vmem(12),
+        out_shape=[tall, tall, pltpu.VMEM((cx + 1, cy + 1, 8, 128), F32)] + [cells] * 9 + [node] * 2,
+        in_specs=[pl.BlockSpec(memory_space=pltpu.SMEM)] * 2 + vmem(15),
         out_specs=vmem(14),
         scratch_shapes=[buf] * 5 + [bp_buf] + elastic_bufs,
+        compiler_params=pltpu.CompilerParams(vmem_limit_bytes=26 << 20),
         name="first_iteration",
     )(
-        rock_table, z_range, *fields, ends, end_places(4, ZRIM, lambda i: (i * ZRIM, (4 + i) * ZRIM)),
+        rock_table, z_range, below, above, *fields, ends, end_places(z_pieces),
         pressure_start, conductance, source, k_own, k_ends, signs,
     )
 
     def ends_of(a):
         return jnp.concatenate([a[..., 128 : 128 + ZR1], a[..., 256 - ZR1 :]], axis=-1)
 
-    p_bf, s_bf = p1.astype(BF), s1.astype(BF)
-    moving = [p_bf[..., :128], s_bf[..., :128], lane_pad(jnp.concatenate([ends_of(p_bf), ends_of(s_bf)], axis=-1))]
+    parts = [*halves(p1), s1.astype(BF)]
+    moving = [a[..., :128] for a in parts] + [lane_pad(jnp.concatenate([ends_of(a) for a in parts], axis=-1))]
     d_bf = d_pack.astype(BF)
     got = exchange(
         rows_of(*moving, d_bf[:, 1 : 1 + ERIM]),
@@ -547,30 +569,33 @@
         "gy",
         False,
     )
-    shapes = [(cx, cy, 128)] * 3 + [(cx + 1, ERIM, 8, 128)]
+    shapes = [(cx, cy, 128)] * 4 + [(cx + 1, ERIM, 8, 128)]
     low, high = cut_rows(got[0], shapes), cut_rows(got[1], shapes)
-    moving = [jnp.concatenate([low[i], moving[i], high[i]], axis=1) for i in range(3)]
-    d_bf = jnp.concatenate([low[3], d_bf, high[3]], axis=1)
+    moving = [jnp.concatenate([low[i], moving[i], high[i]], axis=1) for i in range(4)]
+    d_bf = jnp.concatenate([low[4], d_bf, high[4]], axis=1)
     got = exchange(
         rows_of(*moving, d_bf[1 : 1 + ERIM]),
         rows_of(*moving, d_bf[cx - ERIM : cx]),
         GX,
         True,
     )
-    shapes = [(cx, ey, 128)] * 3 + [(ERIM, cy + 1 + 2 * ERIM, 8, 128)]
-    low, high = cut_rows(got[0], shapes), cut_rows(got[1], shapes)
-    moving = [jnp.concatenate([low[i], moving[i], high[i]], axis=0) for i in range(3)]
-    d_bf = jnp.concatenate([low[3], d_bf, high[3]], axis=0)
+    planes = len(moving) * cx * ey
+    low, high = (cut_rows(g[planes:], [(ERIM, cy + 1 + 2 * ERIM, 8, 128)])[0] for g in got)
+    below, above = (g.reshape(-1, ey, 128) for g in got)
+    d_bf = jnp.concatenate([low, d_bf, high], axis=0)
+    pieces = [(max(i - 1, 0), ZR1, 2 * i * ZR1, (2 * i + 1) * ZR1) for i in range(3)]
+
     short = jax.ShapeDtypeStruct((cx, cy, cz), F32)
     return pl.pallas_call(
         second_flow,
         out_shape=[short, short],
-        in_specs=vmem(11 + 11),
+        in_specs=vmem(14 + 11),
         out_specs=vmem(2),
         scratch_shapes=[buf] * 4 + [bp_buf] + elastic_bufs,
+        compiler_params=pltpu.CompilerParams(vmem_limit_bytes=26 << 20),
         name="second_iteration",
     )(
-        *moving, end_places(2, ZR1, lambda i: (2 * i * ZR1, (2 * i + 1) * ZR1)), p1, s1,
+        below, above, *moving, end_places(pieces), p1, s1,
         d_bf, d_pack, k_own, k_ends, signs, *static,
     )
 

time: 167 us -> 176 us (1.054)
  local copies, waits for them, and re-layouts: 6.46 us -> 35.6 us
  other arithmetic: 16.8 us -> 4.61 us
  Pallas kernels: 56.1 us -> 45.3 us
  waiting for transfers between devices: 40.1 us -> 45.9 us
  starting transfers between devices: 34.4 us -> 30 us
    unnamed x46 -> x151, local copies, waits for them, and re-layouts: 0.82 us -> 23.3 us
    pallas_call x2, Pallas kernels: 56.1 us -> 45.3 us  [the longest x1 23.4 us: per_device(): pl.pallas_call(first_flow, out_shape=[tall, tall, pltpu.VMEM((cx + 1, cy...]
    concatenate x15 -> x5, other arithmetic: 10.4 us -> 1.46 us  [the longest x1 0.95 us: per_device(): jnp.concatenate([jnp.concatenate([low[..., 32:64], after, high[..., 32:64...]
    ppermute x10, waiting for transfers between devices: 34.7 us -> 40.6 us  [exchange(): return (lax.ppermute(to_high, axis, up), lax.ppermute(to_low, axis, down))]
    ppermute x10, starting transfers between devices: 28.6 us -> 24.2 us  [exchange(): return (lax.ppermute(to_high, axis, up), lax.ppermute(to_low, axis, down))]
    slice x8 -> x14, local copies, waits for them, and re-layouts: 0.86 us -> 3.15 us  [the longest x3 2.16 us: per_device(): a[..., :128]]
    slice x2 -> x3, local copies, waits for them, and re-layouts: 0.16 us -> 2.03 us  [ends_of(): return jnp.concatenate([a[..., 128:128 + ZR1], a[..., 256 - ZR1:]], axis=-1)]
    concatenate x2 -> x5, local copies, waits for them, and re-layouts: 0.12 us -> 1.91 us  [the longest x1 1.5 us: per_device(): jnp.concatenate([ends_of(a) for a in parts], axis=-1)]
  transfers between devices with their start and end apart: 11 -> 11, of which waited for: 9 -> 11; matrix products, arithmetic and copies ran while one was open for 3% -> 4% of each run, Pallas kernels for 0% -> 0%
where the time goes in v1:
time: 176 us; the launch traced here: 173 us
  waiting for transfers between devices  45.9 us (26%)
  Pallas kernels  45.3 us (26%)
  local copies, waits for them, and re-layouts  35.6 us (20%)
  starting transfers between devices  30 us (17%)
  matrix products  6.16 us (4%)
  other arithmetic  4.61 us (3%)
  blocking collectives  3.89 us (2%)
  between operations  1.96 us (1%)
    ppermute x10, waiting for transfers between devices, exchange(): return (lax.ppermute(to_high, axis, up), lax.ppermute(to_low, axis, down))  40.6 us
    ppermute x10, starting transfers between devices, exchange(): return (lax.ppermute(to_high, axis, up), lax.ppermute(to_low, axis, down))  24.2 us
    pallas_call x1, Pallas kernels, per_device(): pl.pallas_call(first_flow, out_shape=[tall, tall, pltpu.VMEM((cx + 1, cy...  23.4 us
    unnamed x151, local copies, waits for them, and re-layouts  23.3 us
    pallas_call x1, Pallas kernels, per_device(): pl.pallas_call(second_flow, out_shape=[short, short], in_specs=vmem(14 +...  21.9 us
    all_to_all x1, starting transfers between devices, exchange_in_order(): lax.all_to_all(parts, axes[k], split_axis=k, concat_axis=k, tiled=True)  5.82 us
    all_to_all x1, waiting for transfers between devices, exchange_in_order(): lax.all_to_all(parts, axes[k], split_axis=k, concat_axis=k, tiled=True)  5.32 us
    dot_general x4, matrix products, per_device(): jnp.einsum('ogrk,km->ogrm', held_blocks[:, :, j], lanes_of[j], preferred_...  4.57 us
  transfers between devices with their start and end apart: 11, of which 11 were waited for; matrix products, arithmetic and copies ran while one was open for 4% of the time, Pallas kernels for 0%

profile of v1, /device:TPU:2, one launch (start us, length us, event | category | flops | bytes accessed | tf_op | source)
XLA Modules:
  0.0 173.5 jit_solution(18085497955310309841)
XLA Ops:
  0.7 1.2 fusion.20
  4.2 1.1 fusion
  5.4 3.9 %all_to_all.10 = bf16[8,2,1,2,24,128]{5,4,3,0,2,1:T(8,128)(2,1)S(1)} all-to-all(bf16[8,2,1,2,24,128]{5,4,3,0,2,1:T(8,128)(2,1)S(1)} %copy.81), channel_id=1, replica_groups=mesh['grp'=4,'gx_0'=4,'gx_1'=2,'gx_2'=2,'gy'=4] {'gx_2'}, dimensions={1} | all-to-all | bytes 393216 | tf_op jit(solution)/shard_map/all_to_all | solution.py:77
  10.0 5.8 %all-to-all-start.1 = ((bf16[8,2,1,2,24,128]{5,4,3,1,2,0:T(8,128)(2,1)}), bf16[8,2,1,2,24,128]{5,4,3,1,2,0:T(8,128)(2,1)S(1)}, u32[]{:S(2)}, u32[]{:S(2)}) async-start(bf16[8,2,1,2,24,128]{5,4,3,1,2,0:T(8,128)(2,1)} %copy.82), calls=%async_computation.1 | async-start | bytes 393216 | tf_op jit(solution)/shard_map/all_to_all | solution.py:77
  17.4 5.3 %all-to-all-done.1 = bf16[8,2,1,2,24,128]{5,4,3,1,2,0:T(8,128)(2,1)S(1)} async-done(((bf16[8,2,1,2,24,128]{5,4,3,1,2,0:T(8,128)(2,1)}), bf16[8,2,1,2,24,128]{5,4,3,1,2,0:T(8,128)(2,1)S(1)}, u32[]{:S(2)}, u32[]{:S(2)}) %all-to-all-start.1) | async-done | bytes 196640 | tf_op jit(solution)/shard_map/all_to_all | solution.py:77
  25.5 5.2 %collective-permute-start = (bf16[576,128]{1,0:T(8,128)(2,1)S(1)}, bf16[576,128]{1,0:T(8,128)(2,1)S(1)}, u32[]{:S(2)}, u32[]{:S(2)}) collective-permute-start(bf16[576,128]{1,0:T(8,128)(2,1)S(1)} %constant_dynamic-update-slice_fusion), channel_id=1, source_target_pairs={{0,1},{1,2},{2,3},{4,5},{5,6},{6,7},{8,9},{9,10},{10,11},{12,13},{... | collective-permute-start | bytes 442376 | tf_op jit(solution)/shard_map/ppermute | solution.py:41
  30.8 1.3 collective-permute-start.1
  32.1 1.2 collective-permute-done
  33.5 8.7 %collective-permute-done.1 = bf16[576,128]{1,0:T(8,128)(2,1)S(1)} collective-permute-done((bf16[576,128]{1,0:T(8,128)(2,1)S(1)}, bf16[576,128]{1,0:T(8,128)(2,1)S(1)}, u32[]{:S(2)}, u32[]{:S(2)}) %collective-permute-start.1) | collective-permute-done | bytes 147488 | tf_op jit(solution)/shard_map/ppermute | solution.py:41
  43.8 3.4 %collective-permute-start.3 = (bf16[1088,128]{1,0:T(8,128)(2,1)S(1)}, bf16[1088,128]{1,0:T(8,128)(2,1)S(1)}, u32[]{:S(2)}, u32[]{:S(2)}) collective-permute-start(bf16[1088,128]{1,0:T(8,128)(2,1)S(1)} %pad_maximum_fusion.6), channel_id=1, source_target_pairs={{0,64},{64,128},{128,192},{1,65},{65,129},{129,193},{2,66},{66,130... | collective-permute-start | bytes 835592 | tf_op jit(solution)/shard_map/ppermute | solution.py:41
  47.3 2.4 %collective-permute-start.2 = (bf16[1088,128]{1,0:T(8,128)(2,1)S(1)}, bf16[1088,128]{1,0:T(8,128)(2,1)S(1)}, u32[]{:S(2)}, u32[]{:S(2)}) collective-permute-start(bf16[1088,128]{1,0:T(8,128)(2,1)S(1)} %get-tuple-element.30), channel_id=1, source_target_pairs={{64,0},{128,64},{192,128},{65,1},{129,65},{193,129},{66,2},{130,66... | collective-permute-start | bytes 835592 | tf_op jit(solution)/shard_map/ppermute | solution.py:41
  50.4 3.6 %collective-permute-done.3 = bf16[1088,128]{1,0:T(8,128)(2,1)S(1)} collective-permute-done((bf16[1088,128]{1,0:T(8,128)(2,1)S(1)}, bf16[1088,128]{1,0:T(8,128)(2,1)S(1)}, u32[]{:S(2)}, u32[]{:S(2)}) %collective-permute-start.3) | collective-permute-done | bytes 278560 | tf_op jit(solution)/shard_map/ppermute | solution.py:41
  54.0 3.1 %collective-permute-done.2 = bf16[1088,128]{1,0:T(8,128)(2,1)S(1)} collective-permute-done((bf16[1088,128]{1,0:T(8,128)(2,1)S(1)}, bf16[1088,128]{1,0:T(8,128)(2,1)S(1)}, u32[]{:S(2)}, u32[]{:S(2)}) %collective-permute-start.2) | collective-permute-done | bytes 278560 | tf_op jit(solution)/shard_map/ppermute | solution.py:41
  61.0 12.3 %collective-permute-done.5 = bf16[2496,128]{1,0:T(8,128)(2,1)S(1)} collective-permute-done((bf16[2496,128]{1,0:T(8,128)(2,1)S(1)}, bf16[2496,128]{1,0:T(8,128)(2,1)S(1)}, u32[]{:S(2)}, u32[]{:S(2)}) %collective-permute-start.5) | collective-permute-done | bytes 639008 | tf_op jit(solution)/shard_map/ppermute | solution.py:41
  76.9 23.4 %first_iteration.1 = (f32[8,8,256]{2,1,0:T(8,128)S(1)}, f32[8,8,256]{2,1,0:T(8,128)S(1)}, f32[9,9,8,128]{3,2,1,0:T(8,128)S(1)}, f32[24,24,256]{2,1,0:T(8,128)S(1...) custom-call(f32[5,4]{1,0:T(8,128)S(1)} %copy.106.table, ...), custom_call_target="tpu_custom_call" | custom-call | tf_op jit(solution)/shard_map/first_iteration/pallas_call | solution.py:547
  113.5 1.5 concatenate.167
  115.0 1.5 constant_dynamic-update-slice_fusion.46
  118.1 1.3 collective-permute-start.7
  122.3 5.5 %collective-permute-start.6 = (bf16[472,128]{1,0:T(8,128)(2,1)S(1)}, bf16[472,128]{1,0:T(8,128)(2,1)S(1)}, u32[]{:S(2)}, u32[]{:S(2)}) collective-permute-start(bf16[472,128]{1,0:T(8,128)(2,1)S(1)} %constant_dynamic-update-slice_fusion.40), channel_id=1, source_target_pairs={{0,1},{1,2},{2,3},{4,5},{5,6},{6,7},{8,9},{9,10},{10,11},{12,13},{... | collective-permute-start | bytes 362504 | tf_op jit(solution)/shard_map/ppermute | solution.py:41
  128.6 1.6 collective-permute-done.6
  130.4 4.2 %collective-permute-start.9 = (bf16[1128,128]{1,0:T(8,128)(2,1)S(1)}, bf16[1128,128]{1,0:T(8,128)(2,1)S(1)}, u32[]{:S(2)}, u32[]{:S(2)}) collective-permute-start(bf16[1128,128]{1,0:T(8,128)(2,1)S(1)} %constant_dynamic-update-slice_fusion.55), channel_id=1, source_target_pairs={{4,0},{8,4},{12,8},{16,12},{20,16},{24,20},{28,24},{32,28},{36,32}... | collective-permute-start | bytes 866312 | tf_op jit(solution)/shard_map/ppermute | solution.py:41
  134.7 6.4 %collective-permute-done.9 = bf16[1128,128]{1,0:T(8,128)(2,1)S(1)} collective-permute-done((bf16[1128,128]{1,0:T(8,128)(2,1)S(1)}, bf16[1128,128]{1,0:T(8,128)(2,1)S(1)}, u32[]{:S(2)}, u32[]{:S(2)}) %collective-permute-start.9) | collective-permute-done | bytes 288800 | tf_op jit(solution)/shard_map/ppermute | solution.py:41
  141.1 1.8 %collective-permute-done.8 = bf16[1128,128]{1,0:T(8,128)(2,1)S(1)} collective-permute-done((bf16[1128,128]{1,0:T(8,128)(2,1)S(1)}, bf16[1128,128]{1,0:T(8,128)(2,1)S(1)}, u32[]{:S(2)}, u32[]{:S(2)}) %collective-permute-start.8) | collective-permute-done | bytes 288800 | tf_op jit(solution)/shard_map/ppermute | solution.py:41
  151.5 21.9 %second_iteration.1 = (f32[8,8,128]{2,1,0:T(8,128)}, f32[8,8,128]{2,1,0:T(8,128)}) custom-call(bf16[47,24,128]{2,1,0:T(8,128)(2,1)S(1)} %bitcast.302, bf16[47,24,128]{2,1,0:T(8,128)(2,1)S(1)} %bitcast.301, bf16[8,24,128]{2,1,0:T(8,128)(2,1)S(1)} %pad_maximum_fusion.15.f0, bf16[8,24,128]{2,1,0:T(8,128)(2,1)S(1)} %pad_maximum_fusion.16.f1, ...), custom_call_target="tpu_custom_call" | custom-call | tf_op jit(solution)/shard_map/second_iteration/pallas_call | solution.py:589
  (263 shorter events, 43.9 us)
Async XLA Ops:
  0.7 16.6 %copy-start.50 = (s32[8,8,128]{2,1,0:T(8,128)S(1)}, s32[8,8,128]{2,1,0:T(8,128)}, u32[]{:S(2)}) copy-start(s32[8,8,128]{2,1,0:T(8,128)} %param.25) | copy-start | bytes 98308
  0.7 16.7 %copy-start.58 = (s32[64]{0:T(128)S(1)}, s32[64]{0:T(128)}, u32[]{:S(2)}) copy-start(s32[64]{0:T(128)} %param.21) | copy-start | bytes 772
  1.9 21.5 %copy-start.59 = (bf16[128,32,1]{0,1,2:T(8,128)(2,1)S(1)}, bf16[128,32,1]{0,1,2:T(8,128)(2,1)}, u32[]{:S(2)}) copy-start(bf16[128,32,1]{0,1,2:T(8,128)(2,1)} %constant.207) | copy-start | bytes 24580
  4.2 20.0 %copy-start.53 = (bf16[32,24,1]{0,1,2:T(8,128)(2,1)S(1)}, bf16[32,24,1]{0,1,2:T(8,128)(2,1)}, u32[]{:S(2)}) copy-start(bf16[32,24,1]{0,1,2:T(8,128)(2,1)} %constant.208) | copy-start | bytes 4612
  10.0 12.8 %all-to-all-start.1 = ((bf16[8,2,1,2,24,128]{5,4,3,1,2,0:T(8,128)(2,1)}), bf16[8,2,1,2,24,128]{5,4,3,1,2,0:T(8,128)(2,1)S(1)}, u32[]{:S(2)}, u32[]{:S(2)}) async-start(bf16[8,2,1,2,24,128]{5,4,3,1,2,0:T(8,128)(2,1)} %copy.82), calls=%async_computation.1 | async-start | bytes 393216 | tf_op jit(solution)/shard_map/all_to_all | solution.py:77
  25.5 7.8 %collective-permute-start = (bf16[576,128]{1,0:T(8,128)(2,1)S(1)}, bf16[576,128]{1,0:T(8,128)(2,1)S(1)}, u32[]{:S(2)}, u32[]{:S(2)}) collective-permute-start(bf16[576,128]{1,0:T(8,128)(2,1)S(1)} %constant_dynamic-update-slice_fusion), channel_id=1, source_target_pairs={{0,1},{1,2},{2,3},{4,5},{5,6},{6,7},{8,9},{9,10},{10,11},{12,13},{... | collective-permute-start | bytes 442376 | tf_op jit(solution)/shard_map/ppermute | solution.py:41
  30.8 11.4 %collective-permute-start.1 = (bf16[576,128]{1,0:T(8,128)(2,1)S(1)}, bf16[576,128]{1,0:T(8,128)(2,1)S(1)}, u32[]{:S(2)}, u32[]{:S(2)}) collective-permute-start(bf16[576,128]{1,0:T(8,128)(2,1)S(1)} %constant_dynamic-update-slice_fusion.6), channel_id=1, source_target_pairs={{1,0},{2,1},{3,2},{5,4},{6,5},{7,6},{9,8},{10,9},{11,10},{13,12},{... | collective-permute-start | bytes 442376 | tf_op jit(solution)/shard_map/ppermute | solution.py:41
  43.8 10.2 %collective-permute-start.3 = (bf16[1088,128]{1,0:T(8,128)(2,1)S(1)}, bf16[1088,128]{1,0:T(8,128)(2,1)S(1)}, u32[]{:S(2)}, u32[]{:S(2)}) collective-permute-start(bf16[1088,128]{1,0:T(8,128)(2,1)S(1)} %pad_maximum_fusion.6), channel_id=1, source_target_pairs={{0,64},{64,128},{128,192},{1,65},{65,129},{129,193},{2,66},{66,130... | collective-permute-start | bytes 835592 | tf_op jit(solution)/shard_map/ppermute | solution.py:41
  47.3 9.9 %collective-permute-start.2 = (bf16[1088,128]{1,0:T(8,128)(2,1)S(1)}, bf16[1088,128]{1,0:T(8,128)(2,1)S(1)}, u32[]{:S(2)}, u32[]{:S(2)}) collective-permute-start(bf16[1088,128]{1,0:T(8,128)(2,1)S(1)} %get-tuple-element.30), channel_id=1, source_target_pairs={{64,0},{128,64},{192,128},{65,1},{129,65},{193,129},{66,2},{130,66... | collective-permute-start | bytes 835592 | tf_op jit(solution)/shard_map/ppermute | solution.py:41
  58.9 14.3 %collective-permute-start.5 = (bf16[2496,128]{1,0:T(8,128)(2,1)S(1)}, bf16[2496,128]{1,0:T(8,128)(2,1)S(1)}, u32[]{:S(2)}, u32[]{:S(2)}) collective-permute-start(bf16[2496,128]{1,0:T(8,128)(2,1)S(1)} %constant_dynamic-update-slice_fusion.33), channel_id=1, source_target_pairs={{4,0},{8,4},{12,8},{16,12},{20,16},{24,20},{28,24},{32,28},{36,32}... | collective-permute-start | bytes 1916936 | tf_op jit(solution)/shard_map/ppermute | solution.py:41
  59.5 15.2 %collective-permute-start.4 = (bf16[2496,128]{1,0:T(8,128)(2,1)S(1)}, bf16[2496,128]{1,0:T(8,128)(2,1)S(1)}, u32[]{:S(2)}, u32[]{:S(2)}) collective-permute-start(bf16[2496,128]{1,0:T(8,128)(2,1)S(1)} %constant_dynamic-update-slice_fusion.26), channel_id=1, source_target_pairs={{0,4},{4,8},{8,12},{12,16},{16,20},{20,24},{24,28},{28,32},{32,36}... | collective-permute-start | bytes 1916936 | tf_op jit(solution)/shard_map/ppermute | solution.py:41
  76.9 23.4 %copy-start.34 = (f32[4,8,256]{2,1,0:T(8,128)}, f32[4,8,256]{2,1,0:T(8,128)S(1)}, u32[]{:S(2)}) copy-start(f32[4,8,256]{2,1,0:T(8,128)S(1)} %jit_solution_.3.signs) | copy-start | bytes 98308
  115.0 28.0 %copy-start.1 = (bf16[14,14,32,32]{3,2,1,0:T(8,128)(2,1)S(1)}, bf16[14,14,32,32]{3,2,1,0:T(8,128)(2,1)}, u32[]{:S(2)}) copy-start(bf16[14,14,32,32]{3,2,1,0:T(8,128)(2,1)} %copy-done) | copy-start | bytes 1204228
  115.0 28.0 %copy-start.3 = (f32[13,13,8,256]{3,2,1,0:T(8,128)S(1)}, f32[13,13,8,256]{3,2,1,0:T(8,128)}, u32[]{:S(2)}) copy-start(f32[13,13,8,256]{3,2,1,0:T(8,128)} %copy-done.2) | copy-start | bytes 4153348
  115.0 28.0 %copy-start.5 = (f32[13,13,8,256]{3,2,1,0:T(8,128)S(1)}, f32[13,13,8,256]{3,2,1,0:T(8,128)}, u32[]{:S(2)}) copy-start(f32[13,13,8,256]{3,2,1,0:T(8,128)} %copy-done.4) | copy-start | bytes 4153348
  115.0 28.0 %copy-start.17 = (f32[24,24,256]{2,1,0:T(8,128)S(1)}, f32[24,24,256]{2,1,0:T(8,128)}, u32[]{:S(2)}) copy-start(f32[24,24,256]{2,1,0:T(8,128)} %copy-done.16) | copy-start | bytes 1769476
  115.0 28.0 %copy-start.35 = (f32[4,8,256]{2,1,0:T(8,128)S(1)}, f32[4,8,256]{2,1,0:T(8,128)}, u32[]{:S(2)}) copy-start(f32[4,8,256]{2,1,0:T(8,128)} %copy-done.34) | copy-start | bytes 98308
  115.0 28.0 %copy-start.39 = (f32[8,8,256]{2,1,0:T(8,128)S(1)}, f32[8,8,256]{2,1,0:T(8,128)}, u32[]{:S(2)}) copy-start(f32[8,8,256]{2,1,0:T(8,128)} %copy-done.38) | copy-start | bytes 196612
  115.0 28.0 %copy-start.41 = (f32[8,8,256]{2,1,0:T(8,128)S(1)}, f32[8,8,256]{2,1,0:T(8,128)}, u32[]{:S(2)}) copy-start(f32[8,8,256]{2,1,0:T(8,128)} %copy-done.40) | copy-start | bytes 196612
  115.0 28.0 %copy-start.44 = (bf16[128,256]{1,0:T(8,128)(2,1)S(1)}, bf16[128,256]{1,0:T(8,128)(2,1)}, u32[]{:S(2)}) copy-start(bf16[128,256]{1,0:T(8,128)(2,1)} %constant.171.clone.place) | copy-start | bytes 196612
  118.1 10.4 %collective-permute-start.7 = (bf16[472,128]{1,0:T(8,128)(2,1)}, bf16[472,128]{1,0:T(8,128)(2,1)S(1)}, u32[]{:S(2)}, u32[]{:S(2)}) collective-permute-start(bf16[472,128]{1,0:T(8,128)(2,1)} %constant_dynamic-update-slice_fusion.45), channel_id=1, source_target_pairs={{1,0},{2,1},{3,2},{5,4},{6,5},{7,6},{9,8},{10,9},{11,10},{13,12},{... | collective-permute-start | bytes 362504 | tf_op jit(solution)/shard_map/ppermute | solution.py:41
  122.3 7.9 %collective-permute-start.6 = (bf16[472,128]{1,0:T(8,128)(2,1)S(1)}, bf16[472,128]{1,0:T(8,128)(2,1)S(1)}, u32[]{:S(2)}, u32[]{:S(2)}) collective-permute-start(bf16[472,128]{1,0:T(8,128)(2,1)S(1)} %constant_dynamic-update-slice_fusion.40), channel_id=1, source_target_pairs={{0,1},{1,2},{2,3},{4,5},{5,6},{6,7},{8,9},{9,10},{10,11},{12,13},{... | collective-permute-start | bytes 362504 | tf_op jit(solution)/shard_map/ppermute | solution.py:41
  130.4 10.7 %collective-permute-start.9 = (bf16[1128,128]{1,0:T(8,128)(2,1)S(1)}, bf16[1128,128]{1,0:T(8,128)(2,1)S(1)}, u32[]{:S(2)}, u32[]{:S(2)}) collective-permute-start(bf16[1128,128]{1,0:T(8,128)(2,1)S(1)} %constant_dynamic-update-slice_fusion.55), channel_id=1, source_target_pairs={{4,0},{8,4},{12,8},{16,12},{20,16},{24,20},{28,24},{32,28},{36,32}... | collective-permute-start | bytes 866312 | tf_op jit(solution)/shard_map/ppermute | solution.py:41
  134.6 8.3 %collective-permute-start.8 = (bf16[1128,128]{1,0:T(8,128)(2,1)S(1)}, bf16[1128,128]{1,0:T(8,128)(2,1)S(1)}, u32[]{:S(2)}, u32[]{:S(2)}) collective-permute-start(bf16[1128,128]{1,0:T(8,128)(2,1)S(1)} %constant_dynamic-update-slice_fusion.50), channel_id=1, source_target_pairs={{0,4},{4,8},{8,12},{12,16},{16,20},{20,24},{24,28},{28,32},{32,36}... | collective-permute-start | bytes 866312 | tf_op jit(solution)/shard_map/ppermute | solution.py:41
  (47 other events, 165.7 us)

commit v2 on v1

--- a/solution.py
+++ b/solution.py
@@ -102,7 +102,7 @@
     return pltpu.roll(a, 1, axis)
 
 
-def flow_passes(start, spare, num, tx, ty, ty_low, tz, tz_low, inv_den, biot, load, out):
+def flow_passes(start, spare, num, tx, ty, tz, inv_den, biot, load, out):
     ex = start.shape[0]
     cx, cy, width = out.shape
     for k in range(1, FLOW_PASSES + 1):
@@ -115,8 +115,8 @@
             total = (
                 (num[x] + tx[x - 1] * src[x - 1])
                 + (tx[x] * src[x + 1] + ty[x] * roll_up(mid, 0))
-                + (ty_low[x] * roll_down(mid, 0) + tz[x] * roll_up(mid, 1))
-                + tz_low[x] * roll_down(mid, 1)
+                + (roll_down(ty[x] * mid, 0) + tz[x] * roll_up(mid, 1))
+                + roll_down(tz[x] * mid, 1)
             ) * inv_den[x]
             dst[x] = total
             if k == FLOW_PASSES:
@@ -154,7 +154,7 @@
         last = now
 
 
-def elastic_static(held, k_own, k_ends, free, step, low_x, high_x):
+def elastic_static(held, k_own, k_ends, step, low_x, high_x):
     n = k_own.shape[0]
     eye = (lax.broadcasted_iota(jnp.int32, (64, 32), 0) % 32) == lax.broadcasted_iota(jnp.int32, (64, 32), 1)
     eye = jnp.where(eye, 1.0, 0.0)
@@ -183,7 +183,6 @@
             near = (near[0] + near[1]) + (near[2] + near[3])
             near = near + jnp.where(tile_row() < 4, roll_down(near, 1), roll_up(near, 1))
             loose = jnp.where(near > 0, 0.0, 1.0)
-            free[i, j] = loose
             step[i, j] = jnp.where(diag > 0, OMEGA * loose / jnp.where(diag > 0, diag, 1.0), 0.0)
         return carry
 
@@ -209,7 +208,7 @@
     lax.fori_loop(0, n - 1, nodes, 0)
 
 
-def elastic_pass(rim, disp, load, free, step, k_own, k_ends, low_x, high_x, cx):
+def elastic_pass(rim, disp, load, step, k_own, k_ends, low_x, high_x, cx):
     n, m = cx + 2 * rim, ERIM - rim
 
     def bricks(x, carry):
@@ -226,7 +225,8 @@
         for j in range(n - 1):
             residual = load[i + m, j + m] - fold(low_x[i + 1, j] + high_x[i, j])
             at = (i + m + 1, j + m + 1)
-            disp[at] = free[i + m, j + m] * disp[at] + step[i + m, j + m] * residual
+            rate = step[i + m, j + m]
+            disp[at] = jnp.where(rate > 0, disp[at] + rate * residual, 0.0)
         return carry
 
     lax.fori_loop(0, n - 1, nodes, 0)
@@ -251,7 +251,8 @@
 
 def first_flow(
     table, z_range, below, above, f0, f1, f2, f3, f4, ends, place, p_own, c_own, source, k_own, k_ends, signs,
-    out, strain, packed, base, stress, biot, tx, ty, ty_low, tz, tz_low, inv_den, free, step,
+    out, strain, packed, h0, h1, h2, h3, h4, h5, h6, h7,
+    base, stress, biot, tx, ty, tz, inv_den, step, sems,
     start, spare, cond, num, held, bp, disp, load, low_x, high_x,
 ):
     ex, ey = start.shape[0], start.shape[1]
@@ -298,12 +299,10 @@
         t = transmit(c, roll_up(c, 0))
         low = roll_down(t, 0)
         ty[x] = t
-        ty_low[x] = low
         den = inv_den[x] + t + low
         t = transmit(c, roll_up(c, 1))
         low = roll_down(t, 1)
         tz[x] = t
-        tz_low[x] = low
         p = start[x]
         b = base[x] * p + source[x]
         base[x] = b
@@ -312,18 +311,23 @@
         return carry
 
     lax.fori_loop(0, ex, static_terms, 0, unroll=2)
-    flow_passes(start, spare, num, tx, ty, ty_low, tz, tz_low, inv_den, biot, bp, out)
-    elastic_static(held, k_own, k_ends, free, step, low_x, high_x)
+    kept = zip((base, stress, biot, tx, ty, tz, inv_den, step), (h0, h1, h2, h3, h4, h5, h6, h7))
+    saves = [pltpu.make_async_copy(a, h, sems.at[i]) for i, (a, h) in enumerate(kept)]
+    for save in saves[:7]:
+        save.start()
+    flow_passes(start, spare, num, tx, ty, tz, inv_den, biot, bp, out)
+    elastic_static(held, k_own, k_ends, step, low_x, high_x)
+    saves[7].start()
     elastic_load(bp, signs, load)
 
     def first_pass(i, carry):
-        for j in range(free.shape[1]):
+        for j in range(step.shape[1]):
             disp[i + 1, j + 1] = step[i, j] * load[i, j]
         return carry
 
-    lax.fori_loop(0, free.shape[0], first_pass, 0)
+    lax.fori_loop(0, step.shape[0], first_pass, 0)
     for k in range(1, MECH_PASSES):
-        elastic_pass(ERIM - k, disp, load, free, step, k_own, k_ends, low_x, high_x, cx)
+        elastic_pass(ERIM - k, disp, load, step, k_own, k_ends, low_x, high_x, cx)
     elastic_strain(disp, signs, strain)
 
     def pack(i, carry):
@@ -333,15 +337,23 @@
         return carry
 
     lax.fori_loop(0, packed.shape[0], pack, 0)
+    for save in saves:
+        save.wait()
 
 
 def second_flow(
     below, above, f0, f1, f2, ends, place, p_own, s_own, d_ext, d_own, k_own, k_ends, signs,
-    base, stress, biot, tx, ty, ty_low, tz, tz_low, inv_den, free, step,
-    out, strain_out, start, spare, num, strain, bp, disp, load, low_x, high_x,
+    h0, h1, h2, h3, h4, h5, h6, h7,
+    out, strain_out, base, stress, biot, tx, ty, tz, inv_den, step, sems,
+    start, spare, num, strain, bp, disp, load, low_x, high_x,
 ):
     ex = start.shape[0]
     cx, cy = p_own.shape[0], p_own.shape[1]
+
+    kept = zip((h0, h1, h2, h3, h4, h5, h6, h7), (base, stress, biot, tx, ty, tz, inv_den, step))
+    loads = [pltpu.make_async_copy(h, a, sems.at[i]) for i, (h, a) in enumerate(kept)]
+    for one_load in loads:
+        one_load.start()
 
     def gather(plane, offset):
         def one(i, carry):
@@ -361,13 +373,18 @@
     start[RIM : RIM + cx, RIM : RIM + cy, :] = p_own[...]
     strain[RIM : RIM + cx, RIM : RIM + cy, :] = s_own[...]
 
+    for one_load in loads[:7]:
+        one_load.wait()
+
     def numerator(x, carry):
         num[x] = base[x] + stress[x] * start[x] - biot[x] * strain[x]
         return carry
 
     lax.fori_loop(2, ex - 2, numerator, 0, unroll=2)
-    flow_passes(start, spare, num, tx, ty, ty_low, tz, tz_low, inv_den, biot, bp, out)
+    flow_passes(start, spare, num, tx, ty, tz, inv_den, biot, bp, out)
     elastic_load(bp, signs, load)
+
+    loads[7].wait()
 
     def unpacked(d):
         wide = jnp.concatenate([d, pltpu.roll(d, 4, 0)], axis=1)
@@ -387,8 +404,17 @@
 
     lax.fori_loop(0, d_own.shape[0], unpack_own, 0)
     for k in range(MECH_PASSES):
-        elastic_pass(ERIM - k, disp, load, free, step, k_own, k_ends, low_x, high_x, cx)
+        elastic_pass(ERIM - k, disp, load, step, k_own, k_ends, low_x, high_x, cx)
     elastic_strain(disp, signs, strain_out)
+
+
+def pack_blocks(held, lanes_of, out):
+    def one(g, carry):
+        parts = [jnp.dot(held[4 * g + j], lanes_of[j], preferred_element_type=F32) for j in range(4)]
+        out[g] = ((parts[0] + parts[1]) + (parts[2] + parts[3])).astype(BF)
+        return carry
+
+    lax.fori_loop(0, out.shape[0], one, 0, unroll=4)
 
 
 def vmem(n):
@@ -441,10 +467,15 @@
     for j in range(4):
         lanes_of[j, :, 32 * j : 32 * j + 32] = order.T
     lanes_of = jnp.asarray(lanes_of, BF)
-    held_blocks = stiffness.reshape(count_x, capacity // 4, 4, 24, 24)
-    packed = sum(
-        jnp.einsum("ogrk,km->ogrm", held_blocks[:, :, j], lanes_of[j], preferred_element_type=F32) for j in range(4)
-    ).astype(BF)
+    packed = pl.pallas_call(
+        pack_blocks,
+        out_shape=jax.ShapeDtypeStruct((count_x * (capacity // 4), 24, 128), BF),
+        in_specs=vmem(2),
+        out_specs=vmem(1)[0],
+        compiler_params=pltpu.CompilerParams(vmem_limit_bytes=26 << 20),
+        name="pack_blocks",
+    )(stiffness.reshape(count_x * capacity, 24, 24), lanes_of)
+    packed = packed.reshape(count_x, capacity // 4, 24, 128)
     fetched = core_and_chips(packed, (("gx_0", "gx_1"), "gx_2"), (1, 0), 0, 0)
     groups = fetched.reshape(count_x * (capacity // 4), 24, 128)[owners * (capacity // 4) + brick_rank // 4]
     lane_at = lax.broadcasted_iota(jnp.int32, groups.shape, 2) // 32
@@ -529,12 +560,14 @@
     at_xy = (at_x[:, None, :] * at_y[None, :, :]).reshape(ex * ey, -1)
     at_z = jnp.where(lane[:, None] == jnp.arange(256, dtype=jnp.int32)[None, :], well_rates[:, None], 0.0)
     source = jnp.dot(at_xy, at_z, precision=lax.Precision.HIGHEST).reshape(ex, ey, 256)
-    cells = pltpu.VMEM((ex, ey, 256), F32)
+    cells = pltpu.HBM((ex, ey, 256), F32)
     tall = pltpu.VMEM((cx, cy, 256), F32)
     n = cx + 2 * ERIM
-    node = pltpu.VMEM((n - 1, n - 1, 8, 256), F32)
+    node = pltpu.HBM((n - 1, n - 1, 8, 256), F32)
     buf = pltpu.VMEM((ex, ey, 256), F32)
     bp_buf = pltpu.VMEM((n, ey, 256), F32)
+    hbm = pl.BlockSpec(memory_space=pltpu.HBM)
+    static_bufs = [buf] * 7 + [pltpu.VMEM((n - 1, n - 1, 8, 256), F32), pltpu.SemaphoreType.DMA((8,))]
     elastic_bufs = [
         pltpu.VMEM((n + 1, n + 1, 8, 256), F32),
         pltpu.VMEM((n - 1, n - 1, 8, 256), F32),
@@ -546,11 +579,11 @@
     z_range = jnp.stack([start_z, jnp.int32(total_z)]).astype(jnp.int32)
     p1, s1, d_pack, *static = pl.pallas_call(
         first_flow,
-        out_shape=[tall, tall, pltpu.VMEM((cx + 1, cy + 1, 8, 128), F32)] + [cells] * 9 + [node] * 2,
+        out_shape=[tall, tall, pltpu.VMEM((cx + 1, cy + 1, 8, 128), F32)] + [cells] * 7 + [node],
         in_specs=[pl.BlockSpec(memory_space=pltpu.SMEM)] * 2 + vmem(15),
-        out_specs=vmem(14),
-        scratch_shapes=[buf] * 5 + [bp_buf] + elastic_bufs,
-        compiler_params=pltpu.CompilerParams(vmem_limit_bytes=26 << 20),
+        out_specs=vmem(3) + [hbm] * 8,
+        scratch_shapes=static_bufs + [buf] * 5 + [bp_buf] + elastic_bufs,
+        compiler_params=pltpu.CompilerParams(vmem_limit_bytes=34 << 20),
         name="first_iteration",
     )(
         rock_table, z_range, below, above, *fields, ends, end_places(z_pieces),
@@ -585,14 +618,15 @@
     d_bf = jnp.concatenate([low, d_bf, high], axis=0)
     pieces = [(max(i - 1, 0), ZR1, 2 * i * ZR1, (2 * i + 1) * ZR1) for i in range(3)]
 
+    static = [pltpu.with_memory_space_constraint(a, pltpu.HBM) for a in static]
     short = jax.ShapeDtypeStruct((cx, cy, cz), F32)
     return pl.pallas_call(
         second_flow,
         out_shape=[short, short],
-        in_specs=vmem(14 + 11),
+        in_specs=vmem(14) + [hbm] * 8,
         out_specs=vmem(2),
-        scratch_shapes=[buf] * 4 + [bp_buf] + elastic_bufs,
-        compiler_params=pltpu.CompilerParams(vmem_limit_bytes=26 << 20),
+        scratch_shapes=static_bufs + [buf] * 4 + [bp_buf] + elastic_bufs,
+        compiler_params=pltpu.CompilerParams(vmem_limit_bytes=34 << 20),
         name="second_iteration",
     )(
         below, above, *moving, end_places(pieces), p1, s1,

time: 176 us -> 159 us (0.903)
  local copies, waits for them, and re-layouts: 35.6 us -> 19.9 us
  other arithmetic: 4.61 us -> 8.87 us
  matrix products: 6.16 us -> 2.36 us
  waiting for transfers between devices: 45.9 us -> 42.4 us
  Pallas kernels: 45.3 us -> 47.1 us
    unnamed x151 -> x101, local copies, waits for them, and re-layouts: 23.3 us -> 7.57 us
    all_to_all x1, waiting for transfers between devices: 5.32 us -> 0.01 us  [exchange_in_order(): lax.all_to_all(parts, axes[k], split_axis=k, concat_axis=k, tiled=True)]
    dot_general x4 -> x0, matrix products: 4.57 us -> none  [per_device(): jnp.einsum('ogrk,km->ogrm', held_blocks[:, :, j], lanes_of[j], preferred_...]
    unnamed x5, other arithmetic: 0.7 us -> 2.99 us
    ppermute x10, waiting for transfers between devices: 40.6 us -> 42.4 us  [exchange(): return (lax.ppermute(to_high, axis, up), lax.ppermute(to_low, axis, down))]
    pallas_call x1 -> x2, Pallas kernels: 21.9 us -> 23.8 us  [the longest x1 22.4 us: per_device(): pl.pallas_call(second_flow, out_shape=[short, short], in_specs=vmem(14) +...]
  transfers between devices with their start and end apart: 11 -> 11, of which waited for: 11 -> 9; matrix products, arithmetic and copies ran while one was open for 4% -> 8% of each run, Pallas kernels for 0% -> 0%
where the time goes in v2:
time: 159 us; the launch traced here: 157 us
  Pallas kernels  47.1 us (30%)
  waiting for transfers between devices  42.4 us (27%)
  starting transfers between devices  30.5 us (19%)
  local copies, waits for them, and re-layouts  19.9 us (13%)
  other arithmetic  8.87 us (6%)
  blocking collectives  3.89 us (2%)
  matrix products  2.36 us (1%)
  between operations  1.92 us (1%)
    ppermute x10, waiting for transfers between devices, exchange(): return (lax.ppermute(to_high, axis, up), lax.ppermute(to_low, axis, down))  42.4 us
    ppermute x10, starting transfers between devices, exchange(): return (lax.ppermute(to_high, axis, up), lax.ppermute(to_low, axis, down))  24.7 us
    pallas_call x1, Pallas kernels, per_device(): pl.pallas_call(first_flow, out_shape=[tall, tall, pltpu.VMEM((cx + 1, cy...  23.3 us
    pallas_call x1, Pallas kernels, per_device(): pl.pallas_call(second_flow, out_shape=[short, short], in_specs=vmem(14) +...  22.4 us
    unnamed x101, local copies, waits for them, and re-layouts  7.57 us
    all_to_all x1, starting transfers between devices, exchange_in_order(): lax.all_to_all(parts, axes[k], split_axis=k, concat_axis=k, tiled=True)  5.82 us
    all_to_all x1, blocking collectives, exchange_in_order(): lax.all_to_all(parts, axes[k], split_axis=k, concat_axis=k, tiled=True)  3.89 us
  transfers between devices with their start and end apart: 11, of which 9 were waited for; matrix products, arithmetic and copies ran while one was open for 8% of the time, Pallas kernels for 0%

profile of v2, /device:TPU:2, one launch (start us, length us, event | category | flops | bytes accessed | tf_op | source)
XLA Modules:
  0.0 156.9 jit_solution(7102798443199855091)
XLA Ops:
  2.5 1.4 pack_blocks.1
  3.9 3.9 %all_to_all.10 = bf16[8,2,1,2,24,128]{5,4,3,0,2,1:T(8,128)(2,1)S(1)} all-to-all(bf16[8,2,1,2,24,128]{5,4,3,0,2,1:T(8,128)(2,1)S(1)} %copy.73), channel_id=1, replica_groups=mesh['grp'=4,'gx_0'=4,'gx_1'=2,'gx_2'=2,'gy'=4] {'gx_2'}, dimensions={1} | all-to-all | bytes 393216 | tf_op jit(solution)/shard_map/all_to_all | solution.py:77
  8.5 5.8 %all-to-all-start.1 = ((bf16[8,2,1,2,24,128]{5,4,3,1,2,0:T(8,128)(2,1)}), bf16[8,2,1,2,24,128]{5,4,3,1,2,0:T(8,128)(2,1)S(1)}, u32[]{:S(2)}, u32[]{:S(2)}) async-start(bf16[8,2,1,2,24,128]{5,4,3,1,2,0:T(8,128)(2,1)} %copy.74), calls=%async_computation.1 | async-start | bytes 393216 | tf_op jit(solution)/shard_map/all_to_all | solution.py:77
  20.0 1.4 constant_dynamic-update-slice_fusion.9
  24.4 5.2 %collective-permute-start = (bf16[576,128]{1,0:T(8,128)(2,1)S(1)}, bf16[576,128]{1,0:T(8,128)(2,1)S(1)}, u32[]{:S(2)}, u32[]{:S(2)}) collective-permute-start(bf16[576,128]{1,0:T(8,128)(2,1)S(1)} %constant_dynamic-update-slice_fusion), channel_id=1, source_target_pairs={{0,1},{1,2},{2,3},{4,5},{5,6},{6,7},{8,9},{9,10},{10,11},{12,13},{... | collective-permute-start | bytes 442376 | tf_op jit(solution)/shard_map/ppermute | solution.py:41
  29.7 1.3 collective-permute-start.1
  31.0 1.7 %collective-permute-done = bf16[576,128]{1,0:T(8,128)(2,1)S(1)} collective-permute-done((bf16[576,128]{1,0:T(8,128)(2,1)S(1)}, bf16[576,128]{1,0:T(8,128)(2,1)S(1)}, u32[]{:S(2)}, u32[]{:S(2)}) %collective-permute-start) | collective-permute-done | bytes 147488 | tf_op jit(solution)/shard_map/ppermute | solution.py:41
  32.9 9.1 %collective-permute-done.1 = bf16[576,128]{1,0:T(8,128)(2,1)S(1)} collective-permute-done((bf16[576,128]{1,0:T(8,128)(2,1)S(1)}, bf16[576,128]{1,0:T(8,128)(2,1)S(1)}, u32[]{:S(2)}, u32[]{:S(2)}) %collective-permute-start.1) | collective-permute-done | bytes 147488 | tf_op jit(solution)/shard_map/ppermute | solution.py:41
  43.6 3.4 %collective-permute-start.3 = (bf16[1088,128]{1,0:T(8,128)(2,1)S(1)}, bf16[1088,128]{1,0:T(8,128)(2,1)S(1)}, u32[]{:S(2)}, u32[]{:S(2)}) collective-permute-start(bf16[1088,128]{1,0:T(8,128)(2,1)S(1)} %pad_maximum_fusion.6), channel_id=1, source_target_pairs={{0,64},{64,128},{128,192},{1,65},{65,129},{129,193},{2,66},{66,130... | collective-permute-start | bytes 835592 | tf_op jit(solution)/shard_map/ppermute | solution.py:41
  47.0 2.5 %collective-permute-start.2 = (bf16[1088,128]{1,0:T(8,128)(2,1)S(1)}, bf16[1088,128]{1,0:T(8,128)(2,1)S(1)}, u32[]{:S(2)}, u32[]{:S(2)}) collective-permute-start(bf16[1088,128]{1,0:T(8,128)(2,1)S(1)} %get-tuple-element.24), channel_id=1, source_target_pairs={{64,0},{128,64},{192,128},{65,1},{129,65},{193,129},{66,2},{130,66... | collective-permute-start | bytes 835592 | tf_op jit(solution)/shard_map/ppermute | solution.py:41
  50.2 1.9 %collective-permute-done.3 = bf16[1088,128]{1,0:T(8,128)(2,1)S(1)} collective-permute-done((bf16[1088,128]{1,0:T(8,128)(2,1)S(1)}, bf16[1088,128]{1,0:T(8,128)(2,1)S(1)}, u32[]{:S(2)}, u32[]{:S(2)}) %collective-permute-start.3) | collective-permute-done | bytes 278560 | tf_op jit(solution)/shard_map/ppermute | solution.py:41
  52.1 3.4 %collective-permute-done.2 = bf16[1088,128]{1,0:T(8,128)(2,1)S(1)} collective-permute-done((bf16[1088,128]{1,0:T(8,128)(2,1)S(1)}, bf16[1088,128]{1,0:T(8,128)(2,1)S(1)}, u32[]{:S(2)}, u32[]{:S(2)}) %collective-permute-start.2) | collective-permute-done | bytes 278560 | tf_op jit(solution)/shard_map/ppermute | solution.py:41
  59.3 12.3 %collective-permute-done.5 = bf16[2496,128]{1,0:T(8,128)(2,1)S(1)} collective-permute-done((bf16[2496,128]{1,0:T(8,128)(2,1)S(1)}, bf16[2496,128]{1,0:T(8,128)(2,1)S(1)}, u32[]{:S(2)}, u32[]{:S(2)}) %collective-permute-start.5) | collective-permute-done | bytes 639008 | tf_op jit(solution)/shard_map/ppermute | solution.py:41
  71.9 3.5 %collective-permute-done.4 = bf16[2496,128]{1,0:T(8,128)(2,1)S(1)} collective-permute-done((bf16[2496,128]{1,0:T(8,128)(2,1)S(1)}, bf16[2496,128]{1,0:T(8,128)(2,1)S(1)}, u32[]{:S(2)}, u32[]{:S(2)}) %collective-permute-start.4) | collective-permute-done | bytes 639008 | tf_op jit(solution)/shard_map/ppermute | solution.py:41
  77.7 23.3 %first_iteration.1 = (f32[8,8,256]{2,1,0:T(8,128)S(1)}, f32[8,8,256]{2,1,0:T(8,128)S(1)}, f32[9,9,8,128]{3,2,1,0:T(8,128)S(1)}, f32[24,24,256]{2,1,0:T(8,128)}, ...) custom-call(f32[5,4]{1,0:T(8,128)S(1)} %copy.98.table, ...), custom_call_target="tpu_custom_call" | custom-call | tf_op jit(solution)/shard_map/first_iteration/pallas_call | solution.py:580
  104.4 1.5 concatenate.167
  105.9 1.4 constant_dynamic-update-slice_fusion.46
  109.0 1.3 collective-permute-start.7
  113.2 6.5 %collective-permute-start.6 = (bf16[472,128]{1,0:T(8,128)(2,1)S(1)}, bf16[472,128]{1,0:T(8,128)(2,1)S(1)}, u32[]{:S(2)}, u32[]{:S(2)}) collective-permute-start(bf16[472,128]{1,0:T(8,128)(2,1)S(1)} %constant_dynamic-update-slice_fusion.40), channel_id=1, source_target_pairs={{0,1},{1,2},{2,3},{4,5},{5,6},{6,7},{8,9},{9,10},{10,11},{12,13},{... | collective-permute-start | bytes 362504 | tf_op jit(solution)/shard_map/ppermute | solution.py:41
  119.7 2.4 %collective-permute-done.6 = bf16[472,128]{1,0:T(8,128)(2,1)S(1)} collective-permute-done((bf16[472,128]{1,0:T(8,128)(2,1)S(1)}, bf16[472,128]{1,0:T(8,128)(2,1)S(1)}, u32[]{:S(2)}, u32[]{:S(2)}) %collective-permute-start.6) | collective-permute-done | bytes 120864 | tf_op jit(solution)/shard_map/ppermute | solution.py:41
  122.3 3.6 %collective-permute-start.9 = (bf16[1128,128]{1,0:T(8,128)(2,1)S(1)}, bf16[1128,128]{1,0:T(8,128)(2,1)S(1)}, u32[]{:S(2)}, u32[]{:S(2)}) collective-permute-start(bf16[1128,128]{1,0:T(8,128)(2,1)S(1)} %constant_dynamic-update-slice_fusion.55), channel_id=1, source_target_pairs={{4,0},{8,4},{12,8},{16,12},{20,16},{24,20},{28,24},{32,28},{36,32}... | collective-permute-start | bytes 866312 | tf_op jit(solution)/shard_map/ppermute | solution.py:41
  126.1 5.0 %collective-permute-done.9 = bf16[1128,128]{1,0:T(8,128)(2,1)S(1)} collective-permute-done((bf16[1128,128]{1,0:T(8,128)(2,1)S(1)}, bf16[1128,128]{1,0:T(8,128)(2,1)S(1)}, u32[]{:S(2)}, u32[]{:S(2)}) %collective-permute-start.9) | collective-permute-done | bytes 288800 | tf_op jit(solution)/shard_map/ppermute | solution.py:41
  131.0 3.2 %collective-permute-done.8 = bf16[1128,128]{1,0:T(8,128)(2,1)S(1)} collective-permute-done((bf16[1128,128]{1,0:T(8,128)(2,1)S(1)}, bf16[1128,128]{1,0:T(8,128)(2,1)S(1)}, u32[]{:S(2)}, u32[]{:S(2)}) %collective-permute-start.8) | collective-permute-done | bytes 288800 | tf_op jit(solution)/shard_map/ppermute | solution.py:41
  134.4 22.4 %second_iteration.1 = (f32[8,8,128]{2,1,0:T(8,128)}, f32[8,8,128]{2,1,0:T(8,128)}) custom-call(bf16[47,24,128]{2,1,0:T(8,128)(2,1)S(1)} %bitcast.266, bf16[47,24,128]{2,1,0:T(8,128)(2,1)S(1)} %bitcast.265, bf16[8,24,128]{2,1,0:T(8,128)(2,1)S(1)} %pad_maximum_fusion.15.f0, bf16[8,24,128]{2,1,0:T(8,128)(2,1)S(1)} %pad_maximum_fusion.16.f1, ...), custom_call_target="tpu_custom_call" | custom-call | tf_op jit(solution)/shard_map/second_iteration/pallas_call | solution.py:623
  (210 shorter events, 27.7 us)
Async XLA Ops:
  0.6 21.7 %copy-start.34 = (bf16[128,32,1]{0,1,2:T(8,128)(2,1)S(1)}, bf16[128,32,1]{0,1,2:T(8,128)(2,1)}, u32[]{:S(2)}) copy-start(bf16[128,32,1]{0,1,2:T(8,128)(2,1)} %constant.195) | copy-start | bytes 24580
  0.6 20.9 %copy-start.33 = (s32[64]{0:T(128)S(1)}, s32[64]{0:T(128)}, u32[]{:S(2)}) copy-start(s32[64]{0:T(128)} %param.21) | copy-start | bytes 772
  2.5 18.9 %copy-start.28 = (s32[8,8,128]{2,1,0:T(8,128)S(1)}, s32[8,8,128]{2,1,0:T(8,128)}, u32[]{:S(2)}) copy-start(s32[8,8,128]{2,1,0:T(8,128)} %param.19) | copy-start | bytes 98308
  2.5 18.9 %copy-start.29 = (s32[8,8,128]{2,1,0:T(8,128)S(1)}, s32[8,8,128]{2,1,0:T(8,128)}, u32[]{:S(2)}) copy-start(s32[8,8,128]{2,1,0:T(8,128)} %param.25) | copy-start | bytes 98308
  2.5 20.5 %copy-start.30 = (bf16[32,24,1]{0,1,2:T(8,128)(2,1)S(1)}, bf16[32,24,1]{0,1,2:T(8,128)(2,1)}, u32[]{:S(2)}) copy-start(bf16[32,24,1]{0,1,2:T(8,128)(2,1)} %constant.196) | copy-start | bytes 4612
  8.5 13.1 %all-to-all-start.1 = ((bf16[8,2,1,2,24,128]{5,4,3,1,2,0:T(8,128)(2,1)}), bf16[8,2,1,2,24,128]{5,4,3,1,2,0:T(8,128)(2,1)S(1)}, u32[]{:S(2)}, u32[]{:S(2)}) async-start(bf16[8,2,1,2,24,128]{5,4,3,1,2,0:T(8,128)(2,1)} %copy.74), calls=%async_computation.1 | async-start | bytes 393216 | tf_op jit(solution)/shard_map/all_to_all | solution.py:77
  24.4 8.4 %collective-permute-start = (bf16[576,128]{1,0:T(8,128)(2,1)S(1)}, bf16[576,128]{1,0:T(8,128)(2,1)S(1)}, u32[]{:S(2)}, u32[]{:S(2)}) collective-permute-start(bf16[576,128]{1,0:T(8,128)(2,1)S(1)} %constant_dynamic-update-slice_fusion), channel_id=1, source_target_pairs={{0,1},{1,2},{2,3},{4,5},{5,6},{6,7},{8,9},{9,10},{10,11},{12,13},{... | collective-permute-start | bytes 442376 | tf_op jit(solution)/shard_map/ppermute | solution.py:41
  29.7 12.2 %collective-permute-start.1 = (bf16[576,128]{1,0:T(8,128)(2,1)S(1)}, bf16[576,128]{1,0:T(8,128)(2,1)S(1)}, u32[]{:S(2)}, u32[]{:S(2)}) collective-permute-start(bf16[576,128]{1,0:T(8,128)(2,1)S(1)} %constant_dynamic-update-slice_fusion.6), channel_id=1, source_target_pairs={{1,0},{2,1},{3,2},{5,4},{6,5},{7,6},{9,8},{10,9},{11,10},{13,12},{... | collective-permute-start | bytes 442376 | tf_op jit(solution)/shard_map/ppermute | solution.py:41
  42.1 7.9 %copy-start.4 = (bf16[8,24,128]{2,1,0:T(8,128)(2,1)}, bf16[8,24,128]{2,1,0:T(8,128)(2,1)S(1)}, u32[]{:S(2)}) copy-start(bf16[8,24,128]{2,1,0:T(8,128)(2,1)S(1)} %pad_maximum_fusion.11.f1) | copy-start | bytes 147460
  42.2 7.9 %copy-start.6 = (bf16[8,24,128]{2,1,0:T(8,128)(2,1)}, bf16[8,24,128]{2,1,0:T(8,128)(2,1)S(1)}, u32[]{:S(2)}) copy-start(bf16[8,24,128]{2,1,0:T(8,128)(2,1)S(1)} %pad_maximum_fusion.12.f2) | copy-start | bytes 147460
  43.6 8.5 %collective-permute-start.3 = (bf16[1088,128]{1,0:T(8,128)(2,1)S(1)}, bf16[1088,128]{1,0:T(8,128)(2,1)S(1)}, u32[]{:S(2)}, u32[]{:S(2)}) collective-permute-start(bf16[1088,128]{1,0:T(8,128)(2,1)S(1)} %pad_maximum_fusion.6), channel_id=1, source_target_pairs={{0,64},{64,128},{128,192},{1,65},{65,129},{129,193},{2,66},{66,130... | collective-permute-start | bytes 835592 | tf_op jit(solution)/shard_map/ppermute | solution.py:41
  47.0 8.4 %collective-permute-start.2 = (bf16[1088,128]{1,0:T(8,128)(2,1)S(1)}, bf16[1088,128]{1,0:T(8,128)(2,1)S(1)}, u32[]{:S(2)}, u32[]{:S(2)}) collective-permute-start(bf16[1088,128]{1,0:T(8,128)(2,1)S(1)} %get-tuple-element.24), channel_id=1, source_target_pairs={{64,0},{128,64},{192,128},{65,1},{129,65},{193,129},{66,2},{130,66... | collective-permute-start | bytes 835592 | tf_op jit(solution)/shard_map/ppermute | solution.py:41
  57.3 14.3 %collective-permute-start.5 = (bf16[2496,128]{1,0:T(8,128)(2,1)S(1)}, bf16[2496,128]{1,0:T(8,128)(2,1)S(1)}, u32[]{:S(2)}, u32[]{:S(2)}) collective-permute-start(bf16[2496,128]{1,0:T(8,128)(2,1)S(1)} %constant_dynamic-update-slice_fusion.33), channel_id=1, source_target_pairs={{4,0},{8,4},{12,8},{16,12},{20,16},{24,20},{28,24},{32,28},{36,32}... | collective-permute-start | bytes 1916936 | tf_op jit(solution)/shard_map/ppermute | solution.py:41
  57.8 17.6 %collective-permute-start.4 = (bf16[2496,128]{1,0:T(8,128)(2,1)S(1)}, bf16[2496,128]{1,0:T(8,128)(2,1)S(1)}, u32[]{:S(2)}, u32[]{:S(2)}) collective-permute-start(bf16[2496,128]{1,0:T(8,128)(2,1)S(1)} %constant_dynamic-update-slice_fusion.26), channel_id=1, source_target_pairs={{0,4},{4,8},{8,12},{12,16},{16,20},{20,24},{24,28},{28,32},{32,36}... | collective-permute-start | bytes 1916936 | tf_op jit(solution)/shard_map/ppermute | solution.py:41
  77.7 23.3 %copy-start.13 = (f32[4,8,256]{2,1,0:T(8,128)}, f32[4,8,256]{2,1,0:T(8,128)S(1)}, u32[]{:S(2)}) copy-start(f32[4,8,256]{2,1,0:T(8,128)S(1)} %jit_solution_.3.signs) | copy-start | bytes 98308
  105.9 28.4 %copy-start.1 = (bf16[14,14,32,32]{3,2,1,0:T(8,128)(2,1)S(1)}, bf16[14,14,32,32]{3,2,1,0:T(8,128)(2,1)}, u32[]{:S(2)}) copy-start(bf16[14,14,32,32]{3,2,1,0:T(8,128)(2,1)} %copy-done) | copy-start | bytes 1204228
  105.9 28.4 %copy-start.14 = (f32[4,8,256]{2,1,0:T(8,128)S(1)}, f32[4,8,256]{2,1,0:T(8,128)}, u32[]{:S(2)}) copy-start(f32[4,8,256]{2,1,0:T(8,128)} %copy-done.13) | copy-start | bytes 98308
  105.9 28.4 %copy-start.17 = (f32[8,8,256]{2,1,0:T(8,128)S(1)}, f32[8,8,256]{2,1,0:T(8,128)}, u32[]{:S(2)}) copy-start(f32[8,8,256]{2,1,0:T(8,128)} %copy-done.16) | copy-start | bytes 196612
  105.9 28.4 %copy-start.19 = (f32[8,8,256]{2,1,0:T(8,128)S(1)}, f32[8,8,256]{2,1,0:T(8,128)}, u32[]{:S(2)}) copy-start(f32[8,8,256]{2,1,0:T(8,128)} %copy-done.18) | copy-start | bytes 196612
  105.9 28.4 %copy-start.22 = (bf16[128,256]{1,0:T(8,128)(2,1)S(1)}, bf16[128,256]{1,0:T(8,128)(2,1)}, u32[]{:S(2)}) copy-start(bf16[128,256]{1,0:T(8,128)(2,1)} %constant.171.clone.place) | copy-start | bytes 196612
  109.0 10.7 %collective-permute-start.7 = (bf16[472,128]{1,0:T(8,128)(2,1)}, bf16[472,128]{1,0:T(8,128)(2,1)S(1)}, u32[]{:S(2)}, u32[]{:S(2)}) collective-permute-start(bf16[472,128]{1,0:T(8,128)(2,1)} %constant_dynamic-update-slice_fusion.45), channel_id=1, source_target_pairs={{1,0},{2,1},{3,2},{5,4},{6,5},{7,6},{9,8},{10,9},{11,10},{13,12},{... | collective-permute-start | bytes 362504 | tf_op jit(solution)/shard_map/ppermute | solution.py:41
  113.2 8.9 %collective-permute-start.6 = (bf16[472,128]{1,0:T(8,128)(2,1)S(1)}, bf16[472,128]{1,0:T(8,128)(2,1)S(1)}, u32[]{:S(2)}, u32[]{:S(2)}) collective-permute-start(bf16[472,128]{1,0:T(8,128)(2,1)S(1)} %constant_dynamic-update-slice_fusion.40), channel_id=1, source_target_pairs={{0,1},{1,2},{2,3},{4,5},{5,6},{6,7},{8,9},{9,10},{10,11},{12,13},{... | collective-permute-start | bytes 362504 | tf_op jit(solution)/shard_map/ppermute | solution.py:41
  122.3 8.7 %collective-permute-start.9 = (bf16[1128,128]{1,0:T(8,128)(2,1)S(1)}, bf16[1128,128]{1,0:T(8,128)(2,1)S(1)}, u32[]{:S(2)}, u32[]{:S(2)}) collective-permute-start(bf16[1128,128]{1,0:T(8,128)(2,1)S(1)} %constant_dynamic-update-slice_fusion.55), channel_id=1, source_target_pairs={{4,0},{8,4},{12,8},{16,12},{20,16},{24,20},{28,24},{32,28},{36,32}... | collective-permute-start | bytes 866312 | tf_op jit(solution)/shard_map/ppermute | solution.py:41
  126.0 8.3 %collective-permute-start.8 = (bf16[1128,128]{1,0:T(8,128)(2,1)S(1)}, bf16[1128,128]{1,0:T(8,128)(2,1)S(1)}, u32[]{:S(2)}, u32[]{:S(2)}) collective-permute-start(bf16[1128,128]{1,0:T(8,128)(2,1)S(1)} %constant_dynamic-update-slice_fusion.50), channel_id=1, source_target_pairs={{0,4},{4,8},{8,12},{12,16},{16,20},{20,24},{24,28},{28,32},{32,36}... | collective-permute-start | bytes 866312 | tf_op jit(solution)/shard_map/ppermute | solution.py:41
  (22 other events, 39.5 us)

commit v3 on v2

--- a/solution.py
+++ b/solution.py
@@ -561,7 +561,7 @@
     at_z = jnp.where(lane[:, None] == jnp.arange(256, dtype=jnp.int32)[None, :], well_rates[:, None], 0.0)
     source = jnp.dot(at_xy, at_z, precision=lax.Precision.HIGHEST).reshape(ex, ey, 256)
     cells = pltpu.HBM((ex, ey, 256), F32)
-    tall = pltpu.VMEM((cx, cy, 256), F32)
+    tall = pltpu.HBM((cx, cy, 256), F32)
     n = cx + 2 * ERIM
     node = pltpu.HBM((n - 1, n - 1, 8, 256), F32)
     buf = pltpu.VMEM((ex, ey, 256), F32)
@@ -579,7 +579,7 @@
     z_range = jnp.stack([start_z, jnp.int32(total_z)]).astype(jnp.int32)
     p1, s1, d_pack, *static = pl.pallas_call(
         first_flow,
-        out_shape=[tall, tall, pltpu.VMEM((cx + 1, cy + 1, 8, 128), F32)] + [cells] * 7 + [node],
+        out_shape=[tall, tall, pltpu.HBM((cx + 1, cy + 1, 8, 128), F32)] + [cells] * 7 + [node],
         in_specs=[pl.BlockSpec(memory_space=pltpu.SMEM)] * 2 + vmem(15),
         out_specs=vmem(3) + [hbm] * 8,
         scratch_shapes=static_bufs + [buf] * 5 + [bp_buf] + elastic_bufs,

time: 159 us -> 162 us (1.019)
  other arithmetic: 8.87 us -> 11 us
    unnamed x101 -> x75, local copies, waits for them, and re-layouts: 7.57 us -> 7.71 us
  transfers between devices with their start and end apart: 11 -> 11, of which waited for: 9 -> 10; matrix products, arithmetic and copies ran while one was open for 8% -> 7% of each run, Pallas kernels for 0% -> 0%
where the time goes in v3:
time: 162 us; the launch traced here: 160 us
  Pallas kernels  47.8 us (30%)
  waiting for transfers between devices  42.5 us (26%)
  starting transfers between devices  30.5 us (19%)
  local copies, waits for them, and re-layouts  20 us (12%)
  other arithmetic  11 us (7%)
  blocking collectives  3.89 us (2%)
  matrix products  2.35 us (1%)
  between operations  1.77 us (1%)
    ppermute x10, waiting for transfers between devices, exchange(): return (lax.ppermute(to_high, axis, up), lax.ppermute(to_low, axis, down))  42.2 us
    ppermute x10, starting transfers between devices, exchange(): return (lax.ppermute(to_high, axis, up), lax.ppermute(to_low, axis, down))  24.7 us
    pallas_call x1, Pallas kernels, per_device(): pl.pallas_call(first_flow, out_shape=[tall, tall, pltpu.HBM((cx + 1, cy +...  24.1 us
    pallas_call x1, Pallas kernels, per_device(): pl.pallas_call(second_flow, out_shape=[short, short], in_specs=vmem(14) +...  22.3 us
    unnamed x75, local copies, waits for them, and re-layouts  7.71 us
    all_to_all x1, starting transfers between devices, exchange_in_order(): lax.all_to_all(parts, axes[k], split_axis=k, concat_axis=k, tiled=True)  5.82 us
    all_to_all x1, blocking collectives, exchange_in_order(): lax.all_to_all(parts, axes[k], split_axis=k, concat_axis=k, tiled=True)  3.89 us
  transfers between devices with their start and end apart: 11, of which 10 were waited for; matrix products, arithmetic and copies ran while one was open for 7% of the time, Pallas kernels for 0%

profile of v3, /device:TPU:2, one launch (start us, length us, event | category | flops | bytes accessed | tf_op | source)
XLA Modules:
  0.0 159.9 jit_solution(8591411573957606986)
XLA Ops:
  0.7 1.1 copy-done.3
  2.5 1.4 pack_blocks.1
  3.9 3.9 %all_to_all.10 = bf16[8,2,1,2,24,128]{5,4,3,0,2,1:T(8,128)(2,1)S(1)} all-to-all(bf16[8,2,1,2,24,128]{5,4,3,0,2,1:T(8,128)(2,1)S(1)} %copy.73), channel_id=1, replica_groups=mesh['grp'=4,'gx_0'=4,'gx_1'=2,'gx_2'=2,'gy'=4] {'gx_2'}, dimensions={1} | all-to-all | bytes 393216 | tf_op jit(solution)/shard_map/all_to_all | solution.py:77
  8.5 5.8 %all-to-all-start.1 = ((bf16[8,2,1,2,24,128]{5,4,3,1,2,0:T(8,128)(2,1)}), bf16[8,2,1,2,24,128]{5,4,3,1,2,0:T(8,128)(2,1)S(1)}, u32[]{:S(2)}, u32[]{:S(2)}) async-start(bf16[8,2,1,2,24,128]{5,4,3,1,2,0:T(8,128)(2,1)} %copy.74), calls=%async_computation.1 | async-start | bytes 393216 | tf_op jit(solution)/shard_map/all_to_all | solution.py:77
  24.0 5.2 %collective-permute-start = (bf16[576,128]{1,0:T(8,128)(2,1)S(1)}, bf16[576,128]{1,0:T(8,128)(2,1)S(1)}, u32[]{:S(2)}, u32[]{:S(2)}) collective-permute-start(bf16[576,128]{1,0:T(8,128)(2,1)S(1)} %constant_dynamic-update-slice_fusion), channel_id=1, source_target_pairs={{0,1},{1,2},{2,3},{4,5},{5,6},{6,7},{8,9},{9,10},{10,11},{12,13},{... | collective-permute-start | bytes 442376 | tf_op jit(solution)/shard_map/ppermute | solution.py:41
  29.4 1.3 collective-permute-start.1
  30.7 1.4 collective-permute-done
  32.3 9.1 %collective-permute-done.1 = bf16[576,128]{1,0:T(8,128)(2,1)S(1)} collective-permute-done((bf16[576,128]{1,0:T(8,128)(2,1)S(1)}, bf16[576,128]{1,0:T(8,128)(2,1)S(1)}, u32[]{:S(2)}, u32[]{:S(2)}) %collective-permute-start.1) | collective-permute-done | bytes 147488 | tf_op jit(solution)/shard_map/ppermute | solution.py:41
  43.0 3.4 %collective-permute-start.3 = (bf16[1088,128]{1,0:T(8,128)(2,1)S(1)}, bf16[1088,128]{1,0:T(8,128)(2,1)S(1)}, u32[]{:S(2)}, u32[]{:S(2)}) collective-permute-start(bf16[1088,128]{1,0:T(8,128)(2,1)S(1)} %pad_maximum_fusion.6), channel_id=1, source_target_pairs={{0,64},{64,128},{128,192},{1,65},{65,129},{129,193},{2,66},{66,130... | collective-permute-start | bytes 835592 | tf_op jit(solution)/shard_map/ppermute | solution.py:41
  46.4 2.5 %collective-permute-start.2 = (bf16[1088,128]{1,0:T(8,128)(2,1)S(1)}, bf16[1088,128]{1,0:T(8,128)(2,1)S(1)}, u32[]{:S(2)}, u32[]{:S(2)}) collective-permute-start(bf16[1088,128]{1,0:T(8,128)(2,1)S(1)} %get-tuple-element.24), channel_id=1, source_target_pairs={{64,0},{128,64},{192,128},{65,1},{129,65},{193,129},{66,2},{130,66... | collective-permute-start | bytes 835592 | tf_op jit(solution)/shard_map/ppermute | solution.py:41
  49.5 1.9 %collective-permute-done.3 = bf16[1088,128]{1,0:T(8,128)(2,1)S(1)} collective-permute-done((bf16[1088,128]{1,0:T(8,128)(2,1)S(1)}, bf16[1088,128]{1,0:T(8,128)(2,1)S(1)}, u32[]{:S(2)}, u32[]{:S(2)}) %collective-permute-start.3) | collective-permute-done | bytes 278560 | tf_op jit(solution)/shard_map/ppermute | solution.py:41
  51.4 3.4 %collective-permute-done.2 = bf16[1088,128]{1,0:T(8,128)(2,1)S(1)} collective-permute-done((bf16[1088,128]{1,0:T(8,128)(2,1)S(1)}, bf16[1088,128]{1,0:T(8,128)(2,1)S(1)}, u32[]{:S(2)}, u32[]{:S(2)}) %collective-permute-start.2) | collective-permute-done | bytes 278560 | tf_op jit(solution)/shard_map/ppermute | solution.py:41
  58.7 12.3 %collective-permute-done.5 = bf16[2496,128]{1,0:T(8,128)(2,1)S(1)} collective-permute-done((bf16[2496,128]{1,0:T(8,128)(2,1)S(1)}, bf16[2496,128]{1,0:T(8,128)(2,1)S(1)}, u32[]{:S(2)}, u32[]{:S(2)}) %collective-permute-start.5) | collective-permute-done | bytes 639008 | tf_op jit(solution)/shard_map/ppermute | solution.py:41
  71.2 3.5 %collective-permute-done.4 = bf16[2496,128]{1,0:T(8,128)(2,1)S(1)} collective-permute-done((bf16[2496,128]{1,0:T(8,128)(2,1)S(1)}, bf16[2496,128]{1,0:T(8,128)(2,1)S(1)}, u32[]{:S(2)}, u32[]{:S(2)}) %collective-permute-start.4) | collective-permute-done | bytes 639008 | tf_op jit(solution)/shard_map/ppermute | solution.py:41
  76.7 24.1 %first_iteration.1 = (f32[8,8,256]{2,1,0:T(8,128)}, f32[8,8,256]{2,1,0:T(8,128)}, f32[9,9,8,128]{3,2,1,0:T(8,128)}, f32[24,24,256]{2,1,0:T(8,128)}, f32[24,24,25...) custom-call(f32[5,4]{1,0:T(8,128)S(1)} %copy.98.table, ...), custom_call_target="tpu_custom_call" | custom-call | tf_op jit(solution)/shard_map/first_iteration/pallas_call | solution.py:580
  106.4 1.5 concatenate.167
  107.9 1.4 constant_dynamic-update-slice_fusion.46
  112.0 1.3 collective-permute-start.7
  116.1 6.5 %collective-permute-start.6 = (bf16[472,128]{1,0:T(8,128)(2,1)S(1)}, bf16[472,128]{1,0:T(8,128)(2,1)S(1)}, u32[]{:S(2)}, u32[]{:S(2)}) collective-permute-start(bf16[472,128]{1,0:T(8,128)(2,1)S(1)} %constant_dynamic-update-slice_fusion.40), channel_id=1, source_target_pairs={{0,1},{1,2},{2,3},{4,5},{5,6},{6,7},{8,9},{9,10},{10,11},{12,13},{... | collective-permute-start | bytes 362504 | tf_op jit(solution)/shard_map/ppermute | solution.py:41
  122.7 2.4 %collective-permute-done.6 = bf16[472,128]{1,0:T(8,128)(2,1)S(1)} collective-permute-done((bf16[472,128]{1,0:T(8,128)(2,1)S(1)}, bf16[472,128]{1,0:T(8,128)(2,1)S(1)}, u32[]{:S(2)}, u32[]{:S(2)}) %collective-permute-start.6) | collective-permute-done | bytes 120864 | tf_op jit(solution)/shard_map/ppermute | solution.py:41
  125.3 3.7 %collective-permute-start.9 = (bf16[1128,128]{1,0:T(8,128)(2,1)S(1)}, bf16[1128,128]{1,0:T(8,128)(2,1)S(1)}, u32[]{:S(2)}, u32[]{:S(2)}) collective-permute-start(bf16[1128,128]{1,0:T(8,128)(2,1)S(1)} %constant_dynamic-update-slice_fusion.55), channel_id=1, source_target_pairs={{4,0},{8,4},{12,8},{16,12},{20,16},{24,20},{28,24},{32,28},{36,32}... | collective-permute-start | bytes 866312 | tf_op jit(solution)/shard_map/ppermute | solution.py:41
  129.1 4.9 %collective-permute-done.9 = bf16[1128,128]{1,0:T(8,128)(2,1)S(1)} collective-permute-done((bf16[1128,128]{1,0:T(8,128)(2,1)S(1)}, bf16[1128,128]{1,0:T(8,128)(2,1)S(1)}, u32[]{:S(2)}, u32[]{:S(2)}) %collective-permute-start.9) | collective-permute-done | bytes 288800 | tf_op jit(solution)/shard_map/ppermute | solution.py:41
  134.0 3.2 %collective-permute-done.8 = bf16[1128,128]{1,0:T(8,128)(2,1)S(1)} collective-permute-done((bf16[1128,128]{1,0:T(8,128)(2,1)S(1)}, bf16[1128,128]{1,0:T(8,128)(2,1)S(1)}, u32[]{:S(2)}, u32[]{:S(2)}) %collective-permute-start.8) | collective-permute-done | bytes 288800 | tf_op jit(solution)/shard_map/ppermute | solution.py:41
  137.4 22.3 %second_iteration.1 = (f32[8,8,128]{2,1,0:T(8,128)}, f32[8,8,128]{2,1,0:T(8,128)}) custom-call(bf16[47,24,128]{2,1,0:T(8,128)(2,1)S(1)} %bitcast.266, bf16[47,24,128]{2,1,0:T(8,128)(2,1)S(1)} %bitcast.265, bf16[8,24,128]{2,1,0:T(8,128)(2,1)S(1)} %pad_maximum_fusion.15.f0, bf16[8,24,128]{2,1,0:T(8,128)(2,1)S(1)} %pad_maximum_fusion.16.f1, ...), custom_call_target="tpu_custom_call" | custom-call | tf_op jit(solution)/shard_map/second_iteration/pallas_call | solution.py:623
  (184 shorter events, 30.5 us)
Async XLA Ops:
  0.6 21.3 %copy-start.21 = (bf16[128,32,1]{0,1,2:T(8,128)(2,1)S(1)}, bf16[128,32,1]{0,1,2:T(8,128)(2,1)}, u32[]{:S(2)}) copy-start(bf16[128,32,1]{0,1,2:T(8,128)(2,1)} %constant.195) | copy-start | bytes 24580
  0.6 20.3 %copy-start.20 = (s32[64]{0:T(128)S(1)}, s32[64]{0:T(128)}, u32[]{:S(2)}) copy-start(s32[64]{0:T(128)} %param.21) | copy-start | bytes 772
  2.5 18.3 %copy-start.15 = (s32[8,8,128]{2,1,0:T(8,128)S(1)}, s32[8,8,128]{2,1,0:T(8,128)}, u32[]{:S(2)}) copy-start(s32[8,8,128]{2,1,0:T(8,128)} %param.19) | copy-start | bytes 98308
  2.5 18.4 %copy-start.16 = (s32[8,8,128]{2,1,0:T(8,128)S(1)}, s32[8,8,128]{2,1,0:T(8,128)}, u32[]{:S(2)}) copy-start(s32[8,8,128]{2,1,0:T(8,128)} %param.25) | copy-start | bytes 98308
  2.5 20.2 %copy-start.17 = (bf16[32,24,1]{0,1,2:T(8,128)(2,1)S(1)}, bf16[32,24,1]{0,1,2:T(8,128)(2,1)}, u32[]{:S(2)}) copy-start(bf16[32,24,1]{0,1,2:T(8,128)(2,1)} %constant.196) | copy-start | bytes 4612
  8.5 12.8 %all-to-all-start.1 = ((bf16[8,2,1,2,24,128]{5,4,3,1,2,0:T(8,128)(2,1)}), bf16[8,2,1,2,24,128]{5,4,3,1,2,0:T(8,128)(2,1)S(1)}, u32[]{:S(2)}, u32[]{:S(2)}) async-start(bf16[8,2,1,2,24,128]{5,4,3,1,2,0:T(8,128)(2,1)} %copy.74), calls=%async_computation.1 | async-start | bytes 393216 | tf_op jit(solution)/shard_map/all_to_all | solution.py:77
  24.0 8.1 %collective-permute-start = (bf16[576,128]{1,0:T(8,128)(2,1)S(1)}, bf16[576,128]{1,0:T(8,128)(2,1)S(1)}, u32[]{:S(2)}, u32[]{:S(2)}) collective-permute-start(bf16[576,128]{1,0:T(8,128)(2,1)S(1)} %constant_dynamic-update-slice_fusion), channel_id=1, source_target_pairs={{0,1},{1,2},{2,3},{4,5},{5,6},{6,7},{8,9},{9,10},{10,11},{12,13},{... | collective-permute-start | bytes 442376 | tf_op jit(solution)/shard_map/ppermute | solution.py:41
  29.4 12.0 %collective-permute-start.1 = (bf16[576,128]{1,0:T(8,128)(2,1)S(1)}, bf16[576,128]{1,0:T(8,128)(2,1)S(1)}, u32[]{:S(2)}, u32[]{:S(2)}) collective-permute-start(bf16[576,128]{1,0:T(8,128)(2,1)S(1)} %constant_dynamic-update-slice_fusion.6), channel_id=1, source_target_pairs={{1,0},{2,1},{3,2},{5,4},{6,5},{7,6},{9,8},{10,9},{11,10},{13,12},{... | collective-permute-start | bytes 442376 | tf_op jit(solution)/shard_map/ppermute | solution.py:41
  43.0 8.4 %collective-permute-start.3 = (bf16[1088,128]{1,0:T(8,128)(2,1)S(1)}, bf16[1088,128]{1,0:T(8,128)(2,1)S(1)}, u32[]{:S(2)}, u32[]{:S(2)}) collective-permute-start(bf16[1088,128]{1,0:T(8,128)(2,1)S(1)} %pad_maximum_fusion.6), channel_id=1, source_target_pairs={{0,64},{64,128},{128,192},{1,65},{65,129},{129,193},{2,66},{66,130... | collective-permute-start | bytes 835592 | tf_op jit(solution)/shard_map/ppermute | solution.py:41
  46.4 8.4 %collective-permute-start.2 = (bf16[1088,128]{1,0:T(8,128)(2,1)S(1)}, bf16[1088,128]{1,0:T(8,128)(2,1)S(1)}, u32[]{:S(2)}, u32[]{:S(2)}) collective-permute-start(bf16[1088,128]{1,0:T(8,128)(2,1)S(1)} %get-tuple-element.24), channel_id=1, source_target_pairs={{64,0},{128,64},{192,128},{65,1},{129,65},{193,129},{66,2},{130,66... | collective-permute-start | bytes 835592 | tf_op jit(solution)/shard_map/ppermute | solution.py:41
  56.6 14.3 %collective-permute-start.5 = (bf16[2496,128]{1,0:T(8,128)(2,1)S(1)}, bf16[2496,128]{1,0:T(8,128)(2,1)S(1)}, u32[]{:S(2)}, u32[]{:S(2)}) collective-permute-start(bf16[2496,128]{1,0:T(8,128)(2,1)S(1)} %constant_dynamic-update-slice_fusion.33), channel_id=1, source_target_pairs={{4,0},{8,4},{12,8},{16,12},{20,16},{24,20},{28,24},{32,28},{36,32}... | collective-permute-start | bytes 1916936 | tf_op jit(solution)/shard_map/ppermute | solution.py:41
  57.2 17.6 %collective-permute-start.4 = (bf16[2496,128]{1,0:T(8,128)(2,1)S(1)}, bf16[2496,128]{1,0:T(8,128)(2,1)S(1)}, u32[]{:S(2)}, u32[]{:S(2)}) collective-permute-start(bf16[2496,128]{1,0:T(8,128)(2,1)S(1)} %constant_dynamic-update-slice_fusion.26), channel_id=1, source_target_pairs={{0,4},{4,8},{8,12},{12,16},{16,20},{20,24},{24,28},{28,32},{32,36}... | collective-permute-start | bytes 1916936 | tf_op jit(solution)/shard_map/ppermute | solution.py:41
  76.7 24.1 %copy-start.4 = (f32[4,8,256]{2,1,0:T(8,128)}, f32[4,8,256]{2,1,0:T(8,128)S(1)}, u32[]{:S(2)}) copy-start(f32[4,8,256]{2,1,0:T(8,128)S(1)} %jit_solution_.3.signs) | copy-start | bytes 98308
  100.8 36.5 %copy-start.2 = (f32[9,9,8,128]{3,2,1,0:T(8,128)S(1)}, f32[9,9,8,128]{3,2,1,0:T(8,128)}, u32[]{:S(2)}) copy-start(f32[9,9,8,128]{3,2,1,0:T(8,128)} %get-tuple-element.15.d_own) | copy-start | bytes 995332
  101.7 4.7 %copy-start.14 = (bf16[8,8,256]{2,1,0:T(8,128)(2,1)}, bf16[8,8,256]{2,1,0:T(8,128)(2,1)S(1)}, u32[]{:S(2)}) copy-start(bf16[8,8,256]{2,1,0:T(8,128)(2,1)S(1)} %get-tuple-element.89) | copy-start | bytes 98308
  107.9 29.4 %copy-start.1 = (bf16[14,14,32,32]{3,2,1,0:T(8,128)(2,1)S(1)}, bf16[14,14,32,32]{3,2,1,0:T(8,128)(2,1)}, u32[]{:S(2)}) copy-start(bf16[14,14,32,32]{3,2,1,0:T(8,128)(2,1)} %copy-done) | copy-start | bytes 1204228
  107.9 29.4 %copy-start.5 = (f32[4,8,256]{2,1,0:T(8,128)S(1)}, f32[4,8,256]{2,1,0:T(8,128)}, u32[]{:S(2)}) copy-start(f32[4,8,256]{2,1,0:T(8,128)} %copy-done.4) | copy-start | bytes 98308
  107.9 29.4 %copy-start.7 = (f32[8,8,256]{2,1,0:T(8,128)S(1)}, f32[8,8,256]{2,1,0:T(8,128)}, u32[]{:S(2)}) copy-start(f32[8,8,256]{2,1,0:T(8,128)} %get-tuple-element.13.p_own) | copy-start | bytes 196612
  107.9 29.4 %copy-start.8 = (f32[8,8,256]{2,1,0:T(8,128)S(1)}, f32[8,8,256]{2,1,0:T(8,128)}, u32[]{:S(2)}) copy-start(f32[8,8,256]{2,1,0:T(8,128)} %get-tuple-element.14.s_own) | copy-start | bytes 196612
  107.9 29.4 %copy-start.10 = (bf16[128,256]{1,0:T(8,128)(2,1)S(1)}, bf16[128,256]{1,0:T(8,128)(2,1)}, u32[]{:S(2)}) copy-start(bf16[128,256]{1,0:T(8,128)(2,1)} %constant.171.clone.place) | copy-start | bytes 196612
  112.0 10.7 %collective-permute-start.7 = (bf16[472,128]{1,0:T(8,128)(2,1)}, bf16[472,128]{1,0:T(8,128)(2,1)S(1)}, u32[]{:S(2)}, u32[]{:S(2)}) collective-permute-start(bf16[472,128]{1,0:T(8,128)(2,1)} %constant_dynamic-update-slice_fusion.45), channel_id=1, source_target_pairs={{1,0},{2,1},{3,2},{5,4},{6,5},{7,6},{9,8},{10,9},{11,10},{13,12},{... | collective-permute-start | bytes 362504 | tf_op jit(solution)/shard_map/ppermute | solution.py:41
  116.1 8.9 %collective-permute-start.6 = (bf16[472,128]{1,0:T(8,128)(2,1)S(1)}, bf16[472,128]{1,0:T(8,128)(2,1)S(1)}, u32[]{:S(2)}, u32[]{:S(2)}) collective-permute-start(bf16[472,128]{1,0:T(8,128)(2,1)S(1)} %constant_dynamic-update-slice_fusion.40), channel_id=1, source_target_pairs={{0,1},{1,2},{2,3},{4,5},{5,6},{6,7},{8,9},{9,10},{10,11},{12,13},{... | collective-permute-start | bytes 362504 | tf_op jit(solution)/shard_map/ppermute | solution.py:41
  125.3 8.7 %collective-permute-start.9 = (bf16[1128,128]{1,0:T(8,128)(2,1)S(1)}, bf16[1128,128]{1,0:T(8,128)(2,1)S(1)}, u32[]{:S(2)}, u32[]{:S(2)}) collective-permute-start(bf16[1128,128]{1,0:T(8,128)(2,1)S(1)} %constant_dynamic-update-slice_fusion.55), channel_id=1, source_target_pairs={{4,0},{8,4},{12,8},{16,12},{20,16},{24,20},{28,24},{32,28},{36,32}... | collective-permute-start | bytes 866312 | tf_op jit(solution)/shard_map/ppermute | solution.py:41
  129.0 8.3 %collective-permute-start.8 = (bf16[1128,128]{1,0:T(8,128)(2,1)S(1)}, bf16[1128,128]{1,0:T(8,128)(2,1)S(1)}, u32[]{:S(2)}, u32[]{:S(2)}) collective-permute-start(bf16[1128,128]{1,0:T(8,128)(2,1)S(1)} %constant_dynamic-update-slice_fusion.50), channel_id=1, source_target_pairs={{0,4},{4,8},{8,12},{12,16},{16,20},{20,24},{24,28},{28,32},{32,36}... | collective-permute-start | bytes 866312 | tf_op jit(solution)/shard_map/ppermute | solution.py:41
  (9 other events, 11.7 us)
